TPU v7x, 32 devices: a whole 2x2x4 slice. The times are simulated.
32 devices in a mesh: inst: 2 (over x), qy: 4 (over z), qx: 4 (over y, core).
Axes of the slice: x: 2, y: 2, z: 4, core: 2. Of those that a mesh axis runs over, the one named last changes fastest.
Arguments:
- cost_diag: float32 [8388608], P(('inst', 'qx', 'qy')), parts along dimension 0
- gammas: float32 [6], replicated
- betas: float32 [6], replicated
Outputs:
- output 1: float32 [2], P('inst'), parts along dimension 0
- output 2: float32 [8388608], P(('inst', 'qx', 'qy')), parts along dimension 0
- output 3: float32 [8388608], P(('inst', 'qx', 'qy')), parts along dimension 0
There are 2 independent parts. A program takes and returns all parts, laid end to end along the dimension named above; an argument that names none is the same for every part.
All inputs are finite; a program needn't handle non-finite values.
Results may differ from a plain program's by a relative error of at most 0.001.
Values sent between devices are 32-bit elements.
A program may use at most 1 GiB of HBM per device.

v0:
```python
import math
import jax
import jax.numpy as jnp
from jax import lax
from jax.sharding import PartitionSpec as P

LANES = 128


def quarter_turn(state_pair):
    sign_pair = jnp.array([1.0, -1.0], jnp.float32).reshape(2, 1, 1)
    return jnp.flip(state_pair, axis=0) * sign_pair


def flip_bit(state_pair, qubit_id):
    if qubit_id < 7:
        axis_id = 2
        bit_step = 1 << qubit_id
    else:
        axis_id = 1
        bit_step = 1 << (qubit_id - 7)
    extent = state_pair.shape[axis_id]
    iota_shape = [1, 1, 1]
    iota_shape[axis_id] = extent
    position = lax.broadcasted_iota(jnp.int32, tuple(iota_shape), axis_id)
    bit_set = (position & bit_step) != 0
    return jnp.where(bit_set, jnp.roll(state_pair, bit_step, axis=axis_id),
                     jnp.roll(state_pair, -bit_step, axis=axis_id))


def local_mixer(state_pair, cos_half, sin_half, qubit_ids):
    for qubit_id in qubit_ids:
        partner = flip_bit(state_pair, qubit_id)
        state_pair = cos_half * state_pair + sin_half * quarter_turn(partner)
    return state_pair


def global_mixer(state_pair, cos_half, sin_half, axis_name, axis_size):
    for bit_id in range(int(math.log2(axis_size))):
        bit_step = 1 << bit_id
        perm_pairs = [(source_id, source_id ^ bit_step) for source_id in range(axis_size)]
        partner = lax.ppermute(state_pair, axis_name, perm_pairs)
        state_pair = cos_half * state_pair + sin_half * quarter_turn(partner)
    return state_pair


def solution(mesh):
    size_x = mesh.shape['qx']
    size_y = mesh.shape['qy']
    state_spec = P(('inst', 'qx', 'qy'))

    def device_body(cost_local, gammas, betas):
        local_len = cost_local.shape[0]
        local_qubits = int(math.log2(local_len))
        row_count = local_len // LANES
        cost_rows = cost_local.reshape(row_count, LANES)
        state_pair = jnp.stack([jnp.ones((row_count, LANES), jnp.float32),
                                jnp.zeros((row_count, LANES), jnp.float32)])
        for layer_id in range(gammas.shape[0]):
            phase_angle = gammas[layer_id] * cost_rows
            state_pair = jnp.cos(phase_angle) * state_pair + jnp.sin(phase_angle) * quarter_turn(state_pair)
            cos_half = jnp.cos(0.5 * betas[layer_id])
            sin_half = jnp.sin(0.5 * betas[layer_id])
            state_pair = local_mixer(state_pair, cos_half, sin_half, range(local_qubits))
            state_pair = global_mixer(state_pair, cos_half, sin_half, 'qy', size_y)
            state_pair = global_mixer(state_pair, cos_half, sin_half, 'qx', size_x)
        local_energy = jnp.sum(cost_rows * (state_pair[0] * state_pair[0] + state_pair[1] * state_pair[1]))
        energy = lax.psum(local_energy, ('qx', 'qy')) / (local_len * size_x * size_y)
        return energy.reshape(1), state_pair[0].reshape(local_len), state_pair[1].reshape(local_len)

    return jax.shard_map(device_body, mesh=mesh, in_specs=(state_spec, P(), P()),
                         out_specs=(P('inst'), state_spec, state_spec), check_vma=False)
```

profile of v0, /device:TPU:0, one launch (start us, length us, event | category | flops | bytes accessed | tf_op | source)
XLA Modules:
  0.0 1437.6 jit_solution(7079524078831251686)
XLA Ops:
  0.6 1.6 fusion.205
  2.2 28.2 %cosine_bitcast_fusion.5 = (f32[2048,128]{1,0:T(8,128)}, f32[2048,128]{1,0:T(8,128)}, f32[2048,128]{1,0:T(8,128)}, f32[2048,128]{1,0:T(8,128)}, f32[2048,128]{1,...) fusion(f32[262144]{0:T(1024)} %param.141, ...), kind=kLoop, calls=%fused_computation.260 | loop fusion | flops 1572864 | bytes 13631512 | tf_op jit(solution)/shard_map/cos | solution.py:61
  34.3 1.1 maximum_select_fusion
  37.5 1.1 maximum_select_fusion.1
  41.0 1.1 maximum_select_fusion.2
  43.9 1.5 maximum_select_fusion.3
  47.1 1.1 maximum_select_fusion.4
  49.9 1.1 maximum_select_fusion.5
  68.5 3.2 collective-permute-start
  71.6 45.6 %collective-permute-done = f32[2,2048,128]{2,1,0:T(8,128)S(1)} collective-permute-done((f32[2,2048,128]{2,1,0:T(8,128)S(1)}, f32[2,2048,128]{2,1,0:T(8,128)S(1)}, u32[]{:S(2)}, u32[]{:S(2)}) %collective-permute-start) | collective-permute-done | bytes 2097184 | tf_op jit(solution)/shard_map/ppermute | solution.py:42
  117.6 2.8 collective-permute-start.1
  120.4 89.8 %collective-permute-done.1 = f32[2,2048,128]{2,1,0:T(8,128)S(1)} collective-permute-done((f32[2,2048,128]{2,1,0:T(8,128)S(1)}, f32[2,2048,128]{2,1,0:T(8,128)S(1)}, u32[]{:S(2)}, u32[]{:S(2)}) %collective-permute-start.1) | collective-permute-done | bytes 2097184 | tf_op jit(solution)/shard_map/ppermute | solution.py:42
  210.7 4.1 collective-permute-done.2
  215.2 1.5 collective-permute-start.3
  217.5 45.5 %collective-permute-done.3 = f32[2,2048,128]{2,1,0:T(8,128)S(1)} collective-permute-done((f32[2,2048,128]{2,1,0:T(8,128)S(1)}, f32[2,2048,128]{2,1,0:T(8,128)S(1)}, u32[]{:S(2)}, u32[]{:S(2)}) %collective-permute-start.3) | collective-permute-done | bytes 2097184 | tf_op jit(solution)/shard_map/ppermute | solution.py:42
  265.1 1.1 maximum_select_fusion.16
  268.3 1.1 maximum_select_fusion.17
  271.1 1.1 maximum_select_fusion.18
  274.2 1.1 maximum_select_fusion.19
  277.0 1.1 maximum_select_fusion.20
  279.9 1.1 maximum_select_fusion.21
  285.0 1.5 maximum_select_fusion.23
  299.3 46.3 %collective-permute-done.4 = f32[2,2048,128]{2,1,0:T(8,128)S(1)} collective-permute-done((f32[2,2048,128]{2,1,0:T(8,128)S(1)}, f32[2,2048,128]{2,1,0:T(8,128)S(1)}, u32[]{:S(2)}, u32[]{:S(2)}) %collective-permute-start.4) | collective-permute-done | bytes 2097184 | tf_op jit(solution)/shard_map/ppermute | solution.py:42
  345.9 2.2 collective-permute-start.5
  348.2 89.6 %collective-permute-done.5 = f32[2,2048,128]{2,1,0:T(8,128)S(1)} collective-permute-done((f32[2,2048,128]{2,1,0:T(8,128)S(1)}, f32[2,2048,128]{2,1,0:T(8,128)S(1)}, u32[]{:S(2)}, u32[]{:S(2)}) %collective-permute-start.5) | collective-permute-done | bytes 2097184 | tf_op jit(solution)/shard_map/ppermute | solution.py:42
  438.1 4.1 collective-permute-done.6
  442.7 1.5 collective-permute-start.7
  445.0 45.5 %collective-permute-done.7 = f32[2,2048,128]{2,1,0:T(8,128)S(1)} collective-permute-done((f32[2,2048,128]{2,1,0:T(8,128)S(1)}, f32[2,2048,128]{2,1,0:T(8,128)S(1)}, u32[]{:S(2)}, u32[]{:S(2)}) %collective-permute-start.7) | collective-permute-done | bytes 2097184 | tf_op jit(solution)/shard_map/ppermute | solution.py:42
  492.5 1.1 maximum_select_fusion.32
  495.7 1.1 maximum_select_fusion.33
  512.4 1.5 maximum_select_fusion.39
  526.6 46.4 %collective-permute-done.8 = f32[2,2048,128]{2,1,0:T(8,128)S(1)} collective-permute-done((f32[2,2048,128]{2,1,0:T(8,128)S(1)}, f32[2,2048,128]{2,1,0:T(8,128)S(1)}, u32[]{:S(2)}, u32[]{:S(2)}) %collective-permute-start.8) | collective-permute-done | bytes 2097184 | tf_op jit(solution)/shard_map/ppermute | solution.py:42
  573.3 2.2 collective-permute-start.9
  575.5 89.6 %collective-permute-done.9 = f32[2,2048,128]{2,1,0:T(8,128)S(1)} collective-permute-done((f32[2,2048,128]{2,1,0:T(8,128)S(1)}, f32[2,2048,128]{2,1,0:T(8,128)S(1)}, u32[]{:S(2)}, u32[]{:S(2)}) %collective-permute-start.9) | collective-permute-done | bytes 2097184 | tf_op jit(solution)/shard_map/ppermute | solution.py:42
  665.5 4.1 collective-permute-done.10
  670.1 1.5 collective-permute-start.11
  672.3 45.5 %collective-permute-done.11 = f32[2,2048,128]{2,1,0:T(8,128)S(1)} collective-permute-done((f32[2,2048,128]{2,1,0:T(8,128)S(1)}, f32[2,2048,128]{2,1,0:T(8,128)S(1)}, u32[]{:S(2)}, u32[]{:S(2)}) %collective-permute-start.11) | collective-permute-done | bytes 2097184 | tf_op jit(solution)/shard_map/ppermute | solution.py:42
  719.9 1.1 maximum_select_fusion.48
  731.8 1.1 maximum_select_fusion.52
  739.8 1.5 maximum_select_fusion.55
  753.9 46.4 %collective-permute-done.12 = f32[2,2048,128]{2,1,0:T(8,128)S(1)} collective-permute-done((f32[2,2048,128]{2,1,0:T(8,128)S(1)}, f32[2,2048,128]{2,1,0:T(8,128)S(1)}, u32[]{:S(2)}, u32[]{:S(2)}) %collective-permute-start.12) | collective-permute-done | bytes 2097184 | tf_op jit(solution)/shard_map/ppermute | solution.py:42
  800.7 2.2 collective-permute-start.13
  802.8 89.6 %collective-permute-done.13 = f32[2,2048,128]{2,1,0:T(8,128)S(1)} collective-permute-done((f32[2,2048,128]{2,1,0:T(8,128)S(1)}, f32[2,2048,128]{2,1,0:T(8,128)S(1)}, u32[]{:S(2)}, u32[]{:S(2)}) %collective-permute-start.13) | collective-permute-done | bytes 2097184 | tf_op jit(solution)/shard_map/ppermute | solution.py:42
  892.9 4.1 collective-permute-done.14
  897.4 1.5 collective-permute-start.15
  899.8 45.4 %collective-permute-done.15 = f32[2,2048,128]{2,1,0:T(8,128)S(1)} collective-permute-done((f32[2,2048,128]{2,1,0:T(8,128)S(1)}, f32[2,2048,128]{2,1,0:T(8,128)S(1)}, u32[]{:S(2)}, u32[]{:S(2)}) %collective-permute-start.15) | collective-permute-done | bytes 2097184 | tf_op jit(solution)/shard_map/ppermute | solution.py:42
  947.3 1.1 maximum_select_fusion.64
  967.2 1.5 maximum_select_fusion.71
  981.3 46.4 %collective-permute-done.16 = f32[2,2048,128]{2,1,0:T(8,128)S(1)} collective-permute-done((f32[2,2048,128]{2,1,0:T(8,128)S(1)}, f32[2,2048,128]{2,1,0:T(8,128)S(1)}, u32[]{:S(2)}, u32[]{:S(2)}) %collective-permute-start.16) | collective-permute-done | bytes 2097184 | tf_op jit(solution)/shard_map/ppermute | solution.py:42
  1028.1 2.1 collective-permute-start.17
  1030.2 89.7 %collective-permute-done.17 = f32[2,2048,128]{2,1,0:T(8,128)S(1)} collective-permute-done((f32[2,2048,128]{2,1,0:T(8,128)S(1)}, f32[2,2048,128]{2,1,0:T(8,128)S(1)}, u32[]{:S(2)}, u32[]{:S(2)}) %collective-permute-start.17) | collective-permute-done | bytes 2097184 | tf_op jit(solution)/shard_map/ppermute | solution.py:42
  1120.3 4.1 collective-permute-done.18
  1124.8 1.5 collective-permute-start.19
  1127.1 45.4 %collective-permute-done.19 = f32[2,2048,128]{2,1,0:T(8,128)S(1)} collective-permute-done((f32[2,2048,128]{2,1,0:T(8,128)S(1)}, f32[2,2048,128]{2,1,0:T(8,128)S(1)}, u32[]{:S(2)}, u32[]{:S(2)}) %collective-permute-start.19) | collective-permute-done | bytes 2097184 | tf_op jit(solution)/shard_map/ppermute | solution.py:42
  1174.7 1.1 maximum_select_fusion.80
  1194.5 1.3 maximum_select_fusion.87
  1208.3 46.5 %collective-permute-done.20 = f32[2,2048,128]{2,1,0:T(8,128)S(1)} collective-permute-done((f32[2,2048,128]{2,1,0:T(8,128)S(1)}, f32[2,2048,128]{2,1,0:T(8,128)S(1)}, u32[]{:S(2)}, u32[]{:S(2)}) %collective-permute-start.20) | collective-permute-done | bytes 2097184 | tf_op jit(solution)/shard_map/ppermute | solution.py:42
  1255.1 2.1 collective-permute-start.21
  1257.2 89.7 %collective-permute-done.21 = f32[2,2048,128]{2,1,0:T(8,128)S(1)} collective-permute-done((f32[2,2048,128]{2,1,0:T(8,128)S(1)}, f32[2,2048,128]{2,1,0:T(8,128)S(1)}, u32[]{:S(2)}, u32[]{:S(2)}) %collective-permute-start.21) | collective-permute-done | bytes 2097184 | tf_op jit(solution)/shard_map/ppermute | solution.py:42
  1347.3 4.1 collective-permute-done.22
  1351.8 1.5 collective-permute-start.23
  1353.3 46.3 %collective-permute-done.23 = f32[2,2048,128]{2,1,0:T(8,128)S(1)} collective-permute-done((f32[2,2048,128]{2,1,0:T(8,128)S(1)}, f32[2,2048,128]{2,1,0:T(8,128)S(1)}, u32[]{:S(2)}, u32[]{:S(2)}) %collective-permute-start.23) | collective-permute-done | bytes 2097184 | tf_op jit(solution)/shard_map/ppermute | solution.py:42
  1399.9 2.1 multiply_reduce_fusion
  1402.1 33.3 %psum.7 = f32[]{:T(128)} all-reduce(f32[]{:T(128)} %get-tuple-element.3), channel_id=1, replica_groups=mesh['inst'=2,'qy'=4,'qx'=4] {'qx','qy'}, use_global_device_ids=true, to_apply=%region_1.2 | all-reduce | flops 1 | bytes 8 | tf_op jit(solution)/shard_map/psum | solution.py:68
  (480 shorter events, 194.0 us)
Async XLA Ops:
  2.2 28.2 %copy-start.11 = (f32[2]{0:T(128)S(1)}, f32[2]{0:T(128)}, u32[]{:S(2)}) copy-start(f32[2]{0:T(128)} %constant.17.clone.1) | copy-start | bytes 28
  30.4 0.7 copy-start
  32.1 0.7 copy-start.10
  68.5 48.8 %collective-permute-start = (f32[2,2048,128]{2,1,0:T(8,128)S(1)}, f32[2,2048,128]{2,1,0:T(8,128)S(1)}, u32[]{:S(2)}, u32[]{:S(2)}) collective-permute-start(f32[2,2048,128]{2,1,0:T(8,128)S(1)} %multiply_add_fusion.119), channel_id=1, source_target_pairs={{0,4},{4,0},{8,12},{12,8},{1,5},{5,1},{9,13},{13,9},{2,6},{6,2},{1... | collective-permute-start | bytes 6291464 | tf_op jit(solution)/shard_map/ppermute | solution.py:42
  117.6 92.6 %collective-permute-start.1 = (f32[2,2048,128]{2,1,0:T(8,128)S(1)}, f32[2,2048,128]{2,1,0:T(8,128)S(1)}, u32[]{:S(2)}, u32[]{:S(2)}) collective-permute-start(f32[2,2048,128]{2,1,0:T(8,128)S(1)} %multiply_add_fusion.118), channel_id=1, source_target_pairs={{0,8},{4,12},{8,0},{12,4},{1,9},{5,13},{9,1},{13,5},{2,10},{6,14},... | collective-permute-start | bytes 6291464 | tf_op jit(solution)/shard_map/ppermute | solution.py:42
  210.6 4.2 collective-permute-start.2
  215.2 47.7 %collective-permute-start.3 = (f32[2,2048,128]{2,1,0:T(8,128)S(1)}, f32[2,2048,128]{2,1,0:T(8,128)S(1)}, u32[]{:S(2)}, u32[]{:S(2)}) collective-permute-start(f32[2,2048,128]{2,1,0:T(8,128)S(1)} %multiply_add_fusion.116), channel_id=1, source_target_pairs={{0,2},{1,3},{2,0},{3,1},{4,6},{5,7},{6,4},{7,5},{8,10},{9,11},{10,... | collective-permute-start | bytes 6291464 | tf_op jit(solution)/shard_map/ppermute | solution.py:42
  298.7 46.9 %collective-permute-start.4 = (f32[2,2048,128]{2,1,0:T(8,128)S(1)}, f32[2,2048,128]{2,1,0:T(8,128)S(1)}, u32[]{:S(2)}, u32[]{:S(2)}) collective-permute-start(f32[2,2048,128]{2,1,0:T(8,128)S(1)} %multiply_add_fusion.96), channel_id=1, source_target_pairs={{0,4},{4,0},{8,12},{12,8},{1,5},{5,1},{9,13},{13,9},{2,6},{6,2},{1... | collective-permute-start | bytes 6291464 | tf_op jit(solution)/shard_map/ppermute | solution.py:42
  345.9 91.8 %collective-permute-start.5 = (f32[2,2048,128]{2,1,0:T(8,128)S(1)}, f32[2,2048,128]{2,1,0:T(8,128)S(1)}, u32[]{:S(2)}, u32[]{:S(2)}) collective-permute-start(f32[2,2048,128]{2,1,0:T(8,128)S(1)} %multiply_add_fusion.95), channel_id=1, source_target_pairs={{0,8},{4,12},{8,0},{12,4},{1,9},{5,13},{9,1},{13,5},{2,10},{6,14},... | collective-permute-start | bytes 6291464 | tf_op jit(solution)/shard_map/ppermute | solution.py:42
  438.1 4.2 collective-permute-start.6
  442.7 47.7 %collective-permute-start.7 = (f32[2,2048,128]{2,1,0:T(8,128)S(1)}, f32[2,2048,128]{2,1,0:T(8,128)S(1)}, u32[]{:S(2)}, u32[]{:S(2)}) collective-permute-start(f32[2,2048,128]{2,1,0:T(8,128)S(1)} %multiply_add_fusion.93), channel_id=1, source_target_pairs={{0,2},{1,3},{2,0},{3,1},{4,6},{5,7},{6,4},{7,5},{8,10},{9,11},{10,... | collective-permute-start | bytes 6291464 | tf_op jit(solution)/shard_map/ppermute | solution.py:42
  444.9 45.8 %copy-start.7 = (f32[2048,128]{1,0:T(8,128)S(1)}, f32[2048,128]{1,0:T(8,128)}, u32[]{:S(2)}) copy-start(f32[2048,128]{1,0:T(8,128)} %get-tuple-element.418) | copy-start | bytes 3145732
  445.0 45.8 %copy-start.8 = (f32[2048,128]{1,0:T(8,128)S(1)}, f32[2048,128]{1,0:T(8,128)}, u32[]{:S(2)}) copy-start(f32[2048,128]{1,0:T(8,128)} %get-tuple-element.422) | copy-start | bytes 3145732
  526.1 46.9 %collective-permute-start.8 = (f32[2,2048,128]{2,1,0:T(8,128)S(1)}, f32[2,2048,128]{2,1,0:T(8,128)S(1)}, u32[]{:S(2)}, u32[]{:S(2)}) collective-permute-start(f32[2,2048,128]{2,1,0:T(8,128)S(1)} %multiply_add_fusion.73), channel_id=1, source_target_pairs={{0,4},{4,0},{8,12},{12,8},{1,5},{5,1},{9,13},{13,9},{2,6},{6,2},{1... | collective-permute-start | bytes 6291464 | tf_op jit(solution)/shard_map/ppermute | solution.py:42
  573.3 91.8 %collective-permute-start.9 = (f32[2,2048,128]{2,1,0:T(8,128)S(1)}, f32[2,2048,128]{2,1,0:T(8,128)S(1)}, u32[]{:S(2)}, u32[]{:S(2)}) collective-permute-start(f32[2,2048,128]{2,1,0:T(8,128)S(1)} %multiply_add_fusion.72), channel_id=1, source_target_pairs={{0,8},{4,12},{8,0},{12,4},{1,9},{5,13},{9,1},{13,5},{2,10},{6,14},... | collective-permute-start | bytes 6291464 | tf_op jit(solution)/shard_map/ppermute | solution.py:42
  665.4 4.2 collective-permute-start.10
  670.1 47.7 %collective-permute-start.11 = (f32[2,2048,128]{2,1,0:T(8,128)S(1)}, f32[2,2048,128]{2,1,0:T(8,128)S(1)}, u32[]{:S(2)}, u32[]{:S(2)}) collective-permute-start(f32[2,2048,128]{2,1,0:T(8,128)S(1)} %multiply_add_fusion.70), channel_id=1, source_target_pairs={{0,2},{1,3},{2,0},{3,1},{4,6},{5,7},{6,4},{7,5},{8,10},{9,11},{10,... | collective-permute-start | bytes 6291464 | tf_op jit(solution)/shard_map/ppermute | solution.py:42
  672.3 45.8 %copy-start.5 = (f32[2048,128]{1,0:T(8,128)S(1)}, f32[2048,128]{1,0:T(8,128)}, u32[]{:S(2)}) copy-start(f32[2048,128]{1,0:T(8,128)} %get-tuple-element.417) | copy-start | bytes 3145732
  672.3 45.8 %copy-start.6 = (f32[2048,128]{1,0:T(8,128)S(1)}, f32[2048,128]{1,0:T(8,128)}, u32[]{:S(2)}) copy-start(f32[2048,128]{1,0:T(8,128)} %get-tuple-element.423) | copy-start | bytes 3145732
  753.4 46.9 %collective-permute-start.12 = (f32[2,2048,128]{2,1,0:T(8,128)S(1)}, f32[2,2048,128]{2,1,0:T(8,128)S(1)}, u32[]{:S(2)}, u32[]{:S(2)}) collective-permute-start(f32[2,2048,128]{2,1,0:T(8,128)S(1)} %multiply_add_fusion.50), channel_id=1, source_target_pairs={{0,4},{4,0},{8,12},{12,8},{1,5},{5,1},{9,13},{13,9},{2,6},{6,2},{1... | collective-permute-start | bytes 6291464 | tf_op jit(solution)/shard_map/ppermute | solution.py:42
  800.7 91.8 %collective-permute-start.13 = (f32[2,2048,128]{2,1,0:T(8,128)S(1)}, f32[2,2048,128]{2,1,0:T(8,128)S(1)}, u32[]{:S(2)}, u32[]{:S(2)}) collective-permute-start(f32[2,2048,128]{2,1,0:T(8,128)S(1)} %multiply_add_fusion.49), channel_id=1, source_target_pairs={{0,8},{4,12},{8,0},{12,4},{1,9},{5,13},{9,1},{13,5},{2,10},{6,14},... | collective-permute-start | bytes 6291464 | tf_op jit(solution)/shard_map/ppermute | solution.py:42
  892.8 4.2 collective-permute-start.14
  897.4 47.7 %collective-permute-start.15 = (f32[2,2048,128]{2,1,0:T(8,128)S(1)}, f32[2,2048,128]{2,1,0:T(8,128)S(1)}, u32[]{:S(2)}, u32[]{:S(2)}) collective-permute-start(f32[2,2048,128]{2,1,0:T(8,128)S(1)} %multiply_add_fusion.47), channel_id=1, source_target_pairs={{0,2},{1,3},{2,0},{3,1},{4,6},{5,7},{6,4},{7,5},{8,10},{9,11},{10,... | collective-permute-start | bytes 6291464 | tf_op jit(solution)/shard_map/ppermute | solution.py:42
  899.8 45.8 %copy-start.3 = (f32[2048,128]{1,0:T(8,128)S(1)}, f32[2048,128]{1,0:T(8,128)}, u32[]{:S(2)}) copy-start(f32[2048,128]{1,0:T(8,128)} %get-tuple-element.416) | copy-start | bytes 3145732
  899.8 45.8 %copy-start.4 = (f32[2048,128]{1,0:T(8,128)S(1)}, f32[2048,128]{1,0:T(8,128)}, u32[]{:S(2)}) copy-start(f32[2048,128]{1,0:T(8,128)} %get-tuple-element.424) | copy-start | bytes 3145732
  980.8 46.9 %collective-permute-start.16 = (f32[2,2048,128]{2,1,0:T(8,128)S(1)}, f32[2,2048,128]{2,1,0:T(8,128)S(1)}, u32[]{:S(2)}, u32[]{:S(2)}) collective-permute-start(f32[2,2048,128]{2,1,0:T(8,128)S(1)} %multiply_add_fusion.27), channel_id=1, source_target_pairs={{0,4},{4,0},{8,12},{12,8},{1,5},{5,1},{9,13},{13,9},{2,6},{6,2},{1... | collective-permute-start | bytes 6291464 | tf_op jit(solution)/shard_map/ppermute | solution.py:42
  1028.1 91.8 %collective-permute-start.17 = (f32[2,2048,128]{2,1,0:T(8,128)S(1)}, f32[2,2048,128]{2,1,0:T(8,128)S(1)}, u32[]{:S(2)}, u32[]{:S(2)}) collective-permute-start(f32[2,2048,128]{2,1,0:T(8,128)S(1)} %multiply_add_fusion.26), channel_id=1, source_target_pairs={{0,8},{4,12},{8,0},{12,4},{1,9},{5,13},{9,1},{13,5},{2,10},{6,14},... | collective-permute-start | bytes 6291464 | tf_op jit(solution)/shard_map/ppermute | solution.py:42
  1120.2 4.2 collective-permute-start.18
  1124.8 47.7 %collective-permute-start.19 = (f32[2,2048,128]{2,1,0:T(8,128)S(1)}, f32[2,2048,128]{2,1,0:T(8,128)S(1)}, u32[]{:S(2)}, u32[]{:S(2)}) collective-permute-start(f32[2,2048,128]{2,1,0:T(8,128)S(1)} %multiply_add_fusion.24), channel_id=1, source_target_pairs={{0,2},{1,3},{2,0},{3,1},{4,6},{5,7},{6,4},{7,5},{8,10},{9,11},{10,... | collective-permute-start | bytes 6291464 | tf_op jit(solution)/shard_map/ppermute | solution.py:42
  1127.1 45.8 %copy-start.1 = (f32[2048,128]{1,0:T(8,128)S(1)}, f32[2048,128]{1,0:T(8,128)}, u32[]{:S(2)}) copy-start(f32[2048,128]{1,0:T(8,128)} %get-tuple-element.414) | copy-start | bytes 3145732
  1127.1 45.8 %copy-start.2 = (f32[2048,128]{1,0:T(8,128)S(1)}, f32[2048,128]{1,0:T(8,128)}, u32[]{:S(2)}) copy-start(f32[2048,128]{1,0:T(8,128)} %get-tuple-element.415) | copy-start | bytes 3145732
  1207.9 46.9 %collective-permute-start.20 = (f32[2,2048,128]{2,1,0:T(8,128)S(1)}, f32[2,2048,128]{2,1,0:T(8,128)S(1)}, u32[]{:S(2)}, u32[]{:S(2)}) collective-permute-start(f32[2,2048,128]{2,1,0:T(8,128)S(1)} %multiply_add_fusion.4), channel_id=1, source_target_pairs={{0,4},{4,0},{8,12},{12,8},{1,5},{5,1},{9,13},{13,9},{2,6},{6,2},{1... | collective-permute-start | bytes 6291464 | tf_op jit(solution)/shard_map/ppermute | solution.py:42
  1255.1 91.8 %collective-permute-start.21 = (f32[2,2048,128]{2,1,0:T(8,128)S(1)}, f32[2,2048,128]{2,1,0:T(8,128)S(1)}, u32[]{:S(2)}, u32[]{:S(2)}) collective-permute-start(f32[2,2048,128]{2,1,0:T(8,128)S(1)} %multiply_add_fusion.3), channel_id=1, source_target_pairs={{0,8},{4,12},{8,0},{12,4},{1,9},{5,13},{9,1},{13,5},{2,10},{6,14},... | collective-permute-start | bytes 6291464 | tf_op jit(solution)/shard_map/ppermute | solution.py:42
  1347.2 4.2 collective-permute-start.22
  1351.8 48.1 %copy-start.9 = (f32[262144]{0:T(1024)S(1)}, f32[262144]{0:T(1024)}, u32[]{:S(2)}) copy-start(f32[262144]{0:T(1024)} %param.141) | copy-start | bytes 3145732
  1351.8 47.7 %collective-permute-start.23 = (f32[2,2048,128]{2,1,0:T(8,128)S(1)}, f32[2,2048,128]{2,1,0:T(8,128)S(1)}, u32[]{:S(2)}, u32[]{:S(2)}) collective-permute-start(f32[2,2048,128]{2,1,0:T(8,128)S(1)} %multiply_add_fusion.1), channel_id=1, source_target_pairs={{0,2},{1,3},{2,0},{3,1},{4,6},{5,7},{6,4},{7,5},{8,10},{9,11},{10,... | collective-permute-start | bytes 6291464 | tf_op jit(solution)/shard_map/ppermute | solution.py:42
where the time goes:
time: 1450 us; the launch traced here: 1440 us
  waiting for transfers between devices  1110 us (77%)
  other arithmetic  178 us (12%)
  local copies, waits for them, and re-layouts  73.2 us (5%)
  blocking collectives  33.3 us (2%)
  starting transfers between devices  28.4 us (2%)
    ppermute x24, waiting for transfers between devices, global_mixer(): partner = lax.ppermute(state_pair, axis_name, perm_pairs)  1110 us
    select_n x96, other arithmetic, flip_bit(): jnp.where(bit_set, jnp.roll(state_pair, bit_step, axis=axis_id), jnp.roll...  90.7 us
    slice x192, local copies, waits for them, and re-layouts, flip_bit(): jnp.roll(state_pair, -bit_step, axis=axis_id)  65.4 us
    add x108, other arithmetic, local_mixer(): state_pair = cos_half * state_pair + sin_half * quarter_turn(partner)  41.3 us
    psum x1, blocking collectives, device_body(): lax.psum(local_energy, ('qx', 'qy')) / (local_len * size_x * size_y)  33.3 us
  transfers between devices with their start and end apart: 24, of which 24 were waited for; matrix products, arithmetic and copies ran while one was open for 0% of the time, Pallas kernels for 0%

commit v1 on v0

v1 whole, which is shorter than its diff:
```python
import functools

import jax
import jax.numpy as jnp
from jax import lax
from jax.experimental import pallas as pl
from jax.experimental.pallas import tpu as pltpu
from jax.sharding import PartitionSpec as P

LANES = 128
SUBLANES = 8
BLOCKS = 16
CHUNKS = 8


def flip(x, m):
    return (x // 2 + m // 2) % 2 * 2 + (x + m) % 2


def rx_pair(a, b, c, s):
    (ar, ai), (br, bi) = a, b
    return (c * ar + s * bi, c * ai - s * br), (c * br + s * ai, c * bi - s * ar)


def rx_list(amps, c, s):
    amps = list(amps)
    step = 1
    while step < len(amps):
        for i in range(len(amps)):
            if not i & step:
                amps[i], amps[i + step] = rx_pair(amps[i], amps[i + step], c, s)
        step *= 2
    return amps


def kernel(layers, vregs, total, cost_in, gam, bet, en_out, re_out, im_out,
           cost, trig, recv, work, send, tabs, en_send, en_recv,
           load_sem, csend_sem, crecv_sem, send_sem, recv_sem, esend_sem, erecv_sem, store_sem):
    n = CHUNKS
    half = n // 2
    per = vregs // n
    a, b = lax.axis_index("qx"), lax.axis_index("qy")
    me = a * 4 + b

    def loop(lo, hi, body):
        def step(i, carry):
            body(i)
            return carry

        lax.fori_loop(lo, hi, step, 0)

    def peer(i):
        m = 15 - i
        pa, pb = flip(a, m % 4), flip(b, m // 4)
        return pa * 4 + pb, {"qx": pa, "qy": pb}

    def put(src, dst, send_s, recv_s, dev):
        return pltpu.make_async_remote_copy(src, dst, send_s, recv_s, device_id=dev,
                                            device_id_type=pl.DeviceIdType.MESH)

    def load(k):
        return pltpu.make_async_copy(cost_in.at[:, k], cost.at[0, k], load_sem.at[k])

    loop(0, n, lambda k: load(k).start())
    barrier = pltpu.get_barrier_semaphore()
    loop(0, 15, lambda i: pl.semaphore_signal(barrier, inc=1, device_id=peer(i)[1],
                                              device_id_type=pl.DeviceIdType.MESH))
    pl.semaphore_wait(barrier, 15)

    def share(k):
        load(k).wait()

        def one(i):
            j, dev = peer(i)
            put(cost.at[0, k, j], cost.at[1, k, me], csend_sem.at[k], crecv_sem.at[k], dev).start()

        loop(0, 15, one)
        pltpu.make_async_copy(cost.at[0, k, me], cost.at[1, k, me], crecv_sem.at[k]).start()

    loop(0, n, share)

    def tables(l):
        angle = jnp.full((SUBLANES, LANES), 0.5 * bet[l], jnp.float32)
        tabs[l, 0] = jnp.cos(angle)
        tabs[l, 1] = jnp.sin(angle)

    loop(0, layers, tables)

    def rows(v):
        return pl.ds(v * SUBLANES, SUBLANES)

    def angles(l, lay, k):
        g = gam[l]

        def body(i):
            for v in range(per):
                t = g * cost[lay, k, i, rows(v), :]
                trig[k, 0, i, rows(v), :] = jnp.cos(t)
                trig[k, 1, i, rows(v), :] = jnp.sin(t)

        loop(0, BLOCKS, body)

    def inner(buf, k, l):
        c, s = tabs[l, 0], tabs[l, 1]
        place = [lax.broadcasted_iota(jnp.int32, (SUBLANES, LANES), d) for d in range(2)]

        def partner(v, axis, step):
            size = (SUBLANES, LANES)[axis]
            if 2 * step == size:
                return pltpu.roll(v, step, axis)
            return jnp.where((place[axis] & step) != 0, pltpu.roll(v, step, axis), pltpu.roll(v, size - step, axis))

        def body(i):
            amps = []
            for v in range(per):
                re, im = buf[k, i, 0, rows(v), :], buf[k, i, 1, rows(v), :]
                for axis, bits in ((1, 7), (0, 3)):
                    for q in range(bits):
                        pr, pi = partner(re, axis, 1 << q), partner(im, axis, 1 << q)
                        re, im = c * re + s * pi, c * im - s * pr
                amps.append((re, im))
            for v, (re, im) in enumerate(rx_list(amps, c, s)):
                buf[k, i, 0, rows(v), :] = re
                buf[k, i, 1, rows(v), :] = im

        loop(0, BLOCKS, body)

    def block_bits(l, k, get, dst):
        c, s = tabs[l, 0], tabs[l, 1]
        for v in range(per):
            amps = rx_list([get(i, rows(v)) for i in range(BLOCKS)], c, s)
            for i, (re, im) in enumerate(amps):
                dst[k, i, 0, rows(v), :] = re
                dst[k, i, 1, rows(v), :] = im

    def chunk_pair(k0, k1, l):
        c, s = tabs[l, 0], tabs[l, 1]

        def body(i):
            for v in range(per):
                p0 = work[k0, i, 0, rows(v), :], work[k0, i, 1, rows(v), :]
                p1 = work[k1, i, 0, rows(v), :], work[k1, i, 1, rows(v), :]
                p0, p1 = rx_pair(p0, p1, c, s)
                work[k0, i, 0, rows(v), :] = p0[0]
                work[k0, i, 1, rows(v), :] = p0[1]
                work[k1, i, 0, rows(v), :] = p1[0]
                work[k1, i, 1, rows(v), :] = p1[1]

        loop(0, BLOCKS, body)

    def half_bits(base, l):
        step = 1
        while step < half:
            def pair(i, step=step):
                k0 = base + i // step * 2 * step + i % step
                chunk_pair(k0, k0 + step, l)

            loop(0, half // 2, pair)
            step *= 2

    def ship(k, p):
        def one(i):
            j, dev = peer(i)
            put(send.at[k, j], recv.at[p, k, me], send_sem.at[k], recv_sem.at[p, k], dev).start()

        loop(0, 15, one)
        pltpu.make_async_copy(send.at[k, me], recv.at[p, k, me], recv_sem.at[p, k]).start()

    def sent(k):
        part = send.at[k, pl.ds(0, BLOCKS - 1)]
        pltpu.make_async_copy(part, part, send_sem.at[k]).wait()

    def arrived(k, p):
        pltpu.make_async_copy(recv.at[p, k], recv.at[p, k], recv_sem.at[p, k]).wait()

    def first_phase(k):
        return lambda i, r: (trig[k, 0, i, r, :], -trig[k, 1, i, r, :])

    def next_phase(k):
        def get(i, r):
            re, im = work[k, i, 0, r, :], work[k, i, 1, r, :]
            co, si = trig[k, 0, i, r, :], trig[k, 1, i, r, :]
            return re * co + im * si, im * co - re * si

        return get

    def collect(l, p, with_angles):
        def one(k, with_inner):
            if with_angles:
                angles(l + 1, 1 - p, k)
            arrived(k, p)
            block_bits(l, k, lambda i, r: (recv[p, k, i, 0, r, :], recv[p, k, i, 1, r, :]), work)
            if with_inner:
                inner(work, k, l)

        loop(0, half, lambda k: one(k, True))
        half_bits(0, l)
        loop(half, n, lambda k: one(k, False))
        half_bits(half, l)

    def start(k, with_inner):
        angles(0, 0, k)
        block_bits(0, k, first_phase(k), send)
        if with_inner:
            inner(send, k, 0)
        ship(k, 0)

    loop(0, half, lambda k: start(k, False))
    loop(half, n, lambda k: start(k, True))

    def costs(k):
        pltpu.make_async_copy(cost.at[1, k], cost.at[1, k], crecv_sem.at[k]).wait()
        part = cost.at[0, k, pl.ds(0, BLOCKS - 1)]
        pltpu.make_async_copy(part, part, csend_sem.at[k]).wait()

    loop(0, n, costs)

    def layer(l):
        p = l % 2
        collect(l, p, True)

        def resend(k, late):
            if not late:
                chunk_pair(k, k + half, l)
            sent(k)
            block_bits(l + 1, k, next_phase(k), send)
            if late:
                inner(send, k, l + 1)
            ship(k, 1 - p)

        loop(0, half, lambda k: resend(k, False))
        loop(half, n, lambda k: resend(k, True))

    loop(0, layers - 1, layer)

    last = layers - 1
    collect(last, last % 2, False)

    def store(part, out, k):
        return pltpu.make_async_copy(work.at[k, :, part], out.at[:, k], store_sem.at[part, k])

    def finish(k, acc):
        chunk_pair(k, k + half, last)
        for kk in (k, k + half):
            store(0, re_out, kk).start()
            store(1, im_out, kk).start()

            def add(i, acc, kk=kk):
                for v in range(per):
                    re, im = work[kk, i, 0, rows(v), :], work[kk, i, 1, rows(v), :]
                    acc = acc + cost[0, kk, i, rows(v), :] * (re * re + im * im)
                return acc

            acc = lax.fori_loop(0, BLOCKS, add, acc)
        return acc

    en_send[...] = lax.fori_loop(0, half, finish, jnp.zeros((SUBLANES, LANES), jnp.float32))
    loop(0, 15, lambda i: put(en_send, en_recv.at[me], esend_sem, erecv_sem, peer(i)[1]).start())
    pltpu.make_async_copy(en_send, en_recv.at[me], erecv_sem).start()

    def drain(k):
        sent(k)
        store(0, re_out, k).wait()
        store(1, im_out, k).wait()

    loop(0, n, drain)
    pltpu.make_async_copy(en_recv, en_recv, erecv_sem).wait()
    part = en_recv.at[pl.ds(0, BLOCKS - 1)]
    pltpu.make_async_copy(part, part, esend_sem).wait()
    full = en_recv[0]
    for i in range(1, BLOCKS):
        full = full + en_recv[i]
    en_out[0] = jnp.sum(full) / total


def solution(mesh):
    state_spec = P(("inst", "qx", "qy"))

    def device_body(cost_local, gammas, betas):
        local = cost_local.shape[0]
        vregs = local // (BLOCKS * SUBLANES * LANES)
        layers = gammas.shape[0]
        n = CHUNKS
        r = vregs // n * SUBLANES
        shape = (BLOCKS, n, r, LANES)
        f32 = jnp.float32
        any_spec = pl.BlockSpec(memory_space=pl.ANY)
        smem = pl.BlockSpec(memory_space=pltpu.SMEM)
        dma = pltpu.SemaphoreType.DMA
        energy, out_re, out_im = pl.pallas_call(
            functools.partial(kernel, layers, vregs, float(local * BLOCKS)),
            out_shape=[jax.ShapeDtypeStruct((1,), f32), jax.ShapeDtypeStruct(shape, f32),
                       jax.ShapeDtypeStruct(shape, f32)],
            in_specs=[any_spec, smem, smem],
            out_specs=[smem, any_spec, any_spec],
            scratch_shapes=[
                pltpu.VMEM((2, n, BLOCKS, r, LANES), f32),
                pltpu.VMEM((n, 2, BLOCKS, r, LANES), f32),
                pltpu.VMEM((2, n, BLOCKS, 2, r, LANES), f32),
                pltpu.VMEM((n, BLOCKS, 2, r, LANES), f32),
                pltpu.VMEM((n, BLOCKS, 2, r, LANES), f32),
                pltpu.VMEM((layers, 2, SUBLANES, LANES), f32),
                pltpu.VMEM((SUBLANES, LANES), f32),
                pltpu.VMEM((BLOCKS, SUBLANES, LANES), f32),
                dma((n,)), dma((n,)), dma((n,)), dma((n,)), dma((2, n)), dma, dma, dma((2, n)),
            ],
            compiler_params=pltpu.CompilerParams(collective_id=0, has_side_effects=True),
            name="qaoa",
        )(cost_local.reshape(shape), gammas, betas)
        return energy, out_re.reshape(local), out_im.reshape(local)

    return jax.shard_map(device_body, mesh=mesh, in_specs=(state_spec, P(), P()),
                         out_specs=(P("inst"), state_spec, state_spec), check_vma=False)
```

time: 1450 us -> 514 us (0.35)
  waiting for transfers between devices: 1110 us -> 0 us
  Pallas kernels: 0 us -> 509 us
  other arithmetic: 178 us -> 0 us
  local copies, waits for them, and re-layouts: 73.2 us -> 3.39 us
  blocking collectives: 33.3 us -> 0 us
  starting transfers between devices: 28.4 us -> 0 us
    ppermute x24 -> x0, waiting for transfers between devices: 1110 us -> none  [global_mixer(): partner = lax.ppermute(state_pair, axis_name, perm_pairs)]
    pallas_call x0 -> x1, Pallas kernels: none -> 509 us  [device_body(): pl.pallas_call(functools.partial(kernel, layers, vregs, float(local * BLO...]
    select_n x96 -> x0, other arithmetic: 90.7 us -> none  [flip_bit(): jnp.where(bit_set, jnp.roll(state_pair, bit_step, axis=axis_id), jnp.roll...]
    slice x206 -> x0, local copies, waits for them, and re-layouts: 72.5 us -> none  [the longest x192 65.4 us: flip_bit(): jnp.roll(state_pair, -bit_step, axis=axis_id)]
    add x138 -> x0, other arithmetic: 52.4 us -> none  [the longest x108 41.3 us: local_mixer(): state_pair = cos_half * state_pair + sin_half * quarter_turn(partner)]
    psum x1 -> x0, blocking collectives: 33.3 us -> none  [device_body(): lax.psum(local_energy, ('qx', 'qy')) / (local_len * size_x * size_y)]
    ppermute x24 -> x0, starting transfers between devices: 28.4 us -> none  [global_mixer(): partner = lax.ppermute(state_pair, axis_name, perm_pairs)]
    cos x1 -> x0, other arithmetic: 28.2 us -> none  [device_body(): jnp.cos(phase_angle) * state_pair]
  transfers between devices with their start and end apart: 24 -> 0, of which waited for: 24 -> 0; matrix products, arithmetic and copies ran while one was open for 0% -> 0% of each run, Pallas kernels for 0% -> 0%
where the time goes in v1:
time: 514 us
  Pallas kernels  509 us (99%)
    pallas_call x1, Pallas kernels, device_body(): pl.pallas_call(functools.partial(kernel, layers, vregs, float(local * BLO...  509 us

profile of v1, /device:TPU:0, one launch (start us, length us, event | category | flops | bytes accessed | tf_op | source)
XLA Modules:
  0.0 514.3 jit_solution(5211624513680327744)
XLA Ops:
  0.6 508.5 %qaoa.1 = (f32[1]{0:T(128)}, f32[16,8,16,128]{3,2,1,0:T(8,128)}, f32[16,8,16,128]{3,2,1,0:T(8,128)}) custom-call(f32[16,8,16,128]{3,2,1,0:T(8,128)} %bitcast.3, f32[6]{0:T(128)} %gam.1, f32[6]{0:T(128)} %bet.1), custom_call_target="tpu_custom_call" | custom-call | tf_op jit(solution)/shard_map/qaoa/pallas_call | solution.py:290
  509.8 0.0 copy-start
  509.8 2.4 copy.10
  512.1 0.0 copy-done
  512.1 1.0 copy.11
Async XLA Ops:
  509.8 2.4 copy-start

commit v2 on v1

--- a/solution.py
+++ b/solution.py
@@ -11,6 +11,7 @@
 SUBLANES = 8
 BLOCKS = 16
 CHUNKS = 8
+GROUP = 4
 
 
 def flip(x, m):
@@ -34,7 +35,7 @@
 
 
 def kernel(layers, vregs, total, cost_in, gam, bet, en_out, re_out, im_out,
-           cost, trig, recv, work, send, tabs, en_send, en_recv,
+           cost, trig, recv, work, send, mats, tabs, en_send, en_recv,
            load_sem, csend_sem, crecv_sem, send_sem, recv_sem, esend_sem, erecv_sem, store_sem):
     n = CHUNKS
     half = n // 2
@@ -83,6 +84,22 @@
         angle = jnp.full((SUBLANES, LANES), 0.5 * bet[l], jnp.float32)
         tabs[l, 0] = jnp.cos(angle)
         tabs[l, 1] = jnp.sin(angle)
+        c, s = tabs[l, 0][0:1, :], tabs[l, 1][0:1, :]
+        row = lax.broadcasted_iota(jnp.int32, (LANES, LANES), 0)
+        col = lax.broadcasted_iota(jnp.int32, (LANES, LANES), 1)
+        size = jnp.ones((LANES, LANES), jnp.float32)
+        count = jnp.zeros((LANES, LANES), jnp.int32)
+        for q in range(7):
+            differ = (row & (1 << q)) != (col & (1 << q))
+            size = size * jnp.where(differ, s, c)
+            count = count + jnp.where(differ, 1, 0)
+        turn = count & 3
+        m_re = jnp.where(turn == 0, size, jnp.where(turn == 2, -size, 0.0))
+        m_im = jnp.where(turn == 3, size, jnp.where(turn == 1, -size, 0.0))
+        mats[l, :LANES, :LANES] = m_re
+        mats[l, :LANES, LANES:] = m_im
+        mats[l, LANES:, :LANES] = -m_im
+        mats[l, LANES:, LANES:] = m_re
 
     loop(0, layers, tables)
 
@@ -101,29 +118,34 @@
         loop(0, BLOCKS, body)
 
     def inner(buf, k, l):
+        size = BLOCKS * per * SUBLANES
+        x = jnp.concatenate([buf[k, :, 0].reshape(size, LANES), buf[k, :, 1].reshape(size, LANES)], axis=1)
+        y = jnp.dot(x, mats[l], precision=lax.Precision.HIGHEST, preferred_element_type=jnp.float32)
+        buf[k, :, 0] = y[:, :LANES].reshape(BLOCKS, per * SUBLANES, LANES)
+        buf[k, :, 1] = y[:, LANES:].reshape(BLOCKS, per * SUBLANES, LANES)
         c, s = tabs[l, 0], tabs[l, 1]
-        place = [lax.broadcasted_iota(jnp.int32, (SUBLANES, LANES), d) for d in range(2)]
-
-        def partner(v, axis, step):
-            size = (SUBLANES, LANES)[axis]
-            if 2 * step == size:
-                return pltpu.roll(v, step, axis)
-            return jnp.where((place[axis] & step) != 0, pltpu.roll(v, step, axis), pltpu.roll(v, size - step, axis))
-
-        def body(i):
-            amps = []
-            for v in range(per):
-                re, im = buf[k, i, 0, rows(v), :], buf[k, i, 1, rows(v), :]
-                for axis, bits in ((1, 7), (0, 3)):
-                    for q in range(bits):
-                        pr, pi = partner(re, axis, 1 << q), partner(im, axis, 1 << q)
+        place = lax.broadcasted_iota(jnp.int32, (SUBLANES, LANES), 0)
+
+        def partner(v, step):
+            if 2 * step == SUBLANES:
+                return pltpu.roll(v, step, 0)
+            return jnp.where((place & step) != 0, pltpu.roll(v, step, 0), pltpu.roll(v, SUBLANES - step, 0))
+
+        def body(g):
+            for i in range(GROUP):
+                i = g * GROUP + i
+                amps = []
+                for v in range(per):
+                    re, im = buf[k, i, 0, rows(v), :], buf[k, i, 1, rows(v), :]
+                    for step in (1, 2, 4):
+                        pr, pi = partner(re, step), partner(im, step)
                         re, im = c * re + s * pi, c * im - s * pr
-                amps.append((re, im))
-            for v, (re, im) in enumerate(rx_list(amps, c, s)):
-                buf[k, i, 0, rows(v), :] = re
-                buf[k, i, 1, rows(v), :] = im
-
-        loop(0, BLOCKS, body)
+                    amps.append((re, im))
+                for v, (re, im) in enumerate(rx_list(amps, c, s)):
+                    buf[k, i, 0, rows(v), :] = re
+                    buf[k, i, 1, rows(v), :] = im
+
+        loop(0, BLOCKS // GROUP, body)
 
     def block_bits(l, k, get, dst):
         c, s = tabs[l, 0], tabs[l, 1]
@@ -299,6 +321,7 @@
                 pltpu.VMEM((2, n, BLOCKS, 2, r, LANES), f32),
                 pltpu.VMEM((n, BLOCKS, 2, r, LANES), f32),
                 pltpu.VMEM((n, BLOCKS, 2, r, LANES), f32),
+                pltpu.VMEM((layers, 2 * LANES, 2 * LANES), f32),
                 pltpu.VMEM((layers, 2, SUBLANES, LANES), f32),
                 pltpu.VMEM((SUBLANES, LANES), f32),
                 pltpu.VMEM((BLOCKS, SUBLANES, LANES), f32),

time: 514 us -> 325 us (0.63)
  Pallas kernels: 509 us -> 319 us
    pallas_call x1, Pallas kernels: 509 us -> 319 us  [device_body(): pl.pallas_call(functools.partial(kernel, layers, vregs, float(local * BLO...]
where the time goes in v2:
time: 325 us
  Pallas kernels  319 us (98%)
  local copies, waits for them, and re-layouts  3.39 us (1%)
    pallas_call x1, Pallas kernels, device_body(): pl.pallas_call(functools.partial(kernel, layers, vregs, float(local * BLO...  319 us

profile of v2, /device:TPU:0, one launch (start us, length us, event | category | flops | bytes accessed | tf_op | source)
XLA Modules:
  0.0 324.7 jit_solution(17303694993979314726)
XLA Ops:
  0.6 318.9 %qaoa.1 = (f32[1]{0:T(128)}, f32[16,8,16,128]{3,2,1,0:T(8,128)}, f32[16,8,16,128]{3,2,1,0:T(8,128)}) custom-call(f32[16,8,16,128]{3,2,1,0:T(8,128)} %bitcast.3, f32[6]{0:T(128)} %gam.1, f32[6]{0:T(128)} %bet.1), custom_call_target="tpu_custom_call" | custom-call | tf_op jit(solution)/shard_map/qaoa/pallas_call | solution.py:312
  320.2 0.0 copy-start
  320.2 2.4 copy.10
  322.5 0.0 copy-done
  322.5 1.0 copy.11
Async XLA Ops:
  320.2 2.4 copy-start

commit v3 on v2

v3 whole, which is shorter than its diff:
```python
import functools

import jax
import jax.numpy as jnp
from jax import lax
from jax.experimental import pallas as pl
from jax.experimental.pallas import tpu as pltpu
from jax.sharding import PartitionSpec as P

LANES = 128
SUBLANES = 8
BLOCKS = 16
CHUNKS = 8
GROUPS = ((0, 1), (1, 3), (4, 3), (7, 1))
GROUP = 4


def flip(x, m):
    return (x // 2 + m // 2) % 2 * 2 + (x + m) % 2


def rx_pair(a, b, c, s):
    (ar, ai), (br, bi) = a, b
    return (c * ar + s * bi, c * ai - s * br), (c * br + s * ai, c * bi - s * ar)


def rx_list(amps, c, s):
    amps = list(amps)
    step = 1
    while step < len(amps):
        for i in range(len(amps)):
            if not i & step:
                amps[i], amps[i + step] = rx_pair(amps[i], amps[i + step], c, s)
        step *= 2
    return amps


def kernel(layers, vregs, total, cost_in, gam, bet, en_out, work,
           cost, trig, recv, send, mats, tabs, en_send, en_recv,
           load_sem, csend_sem, crecv_sem, send_sem, recv_sem, esend_sem, erecv_sem):
    n = CHUNKS
    half = n // 2
    per = vregs // n
    a, b = lax.axis_index("qx"), lax.axis_index("qy")
    me = a * 4 + b

    def loop(lo, hi, body):
        def step(i, carry):
            body(i)
            return carry

        lax.fori_loop(lo, hi, step, 0)

    def peer(i):
        m = 15 - i
        pa, pb = flip(a, m % 4), flip(b, m // 4)
        return pa * 4 + pb, {"qx": pa, "qy": pb}

    def put(src, dst, send_s, recv_s, dev):
        return pltpu.make_async_remote_copy(src, dst, send_s, recv_s, device_id=dev,
                                            device_id_type=pl.DeviceIdType.MESH)

    load = pltpu.make_async_copy(cost_in, cost.at[0], load_sem)
    load.start()
    barrier = pltpu.get_barrier_semaphore()
    loop(0, 15, lambda i: pl.semaphore_signal(barrier, inc=1, device_id=peer(i)[1],
                                              device_id_type=pl.DeviceIdType.MESH))
    pl.semaphore_wait(barrier, 15)
    load.wait()

    def share(i):
        j, dev = peer(i)
        put(cost.at[0, j], cost.at[1, me], csend_sem, crecv_sem, dev).start()

    loop(0, 15, share)
    pltpu.make_async_copy(cost.at[0, me], cost.at[1, me], crecv_sem).start()

    def tables(l):
        angle = jnp.full((SUBLANES, LANES), 0.5 * bet[l], jnp.float32)
        tabs[l, 0] = jnp.cos(angle)
        tabs[l, 1] = jnp.sin(angle)
        c, s = tabs[l, 0][0:1, :], tabs[l, 1][0:1, :]
        row = lax.broadcasted_iota(jnp.int32, (LANES, LANES), 0)
        col = lax.broadcasted_iota(jnp.int32, (LANES, LANES), 1)
        size = jnp.ones((LANES, LANES), jnp.float32)
        count = jnp.zeros((LANES, LANES), jnp.int32)
        for q in range(7):
            differ = (row & (1 << q)) != (col & (1 << q))
            size = size * jnp.where(differ, s, c)
            count = count + jnp.where(differ, 1, 0)
        turn = count & 3
        m_re = jnp.where(turn == 0, size, jnp.where(turn == 2, -size, 0.0))
        m_im = jnp.where(turn == 3, size, jnp.where(turn == 1, -size, 0.0))
        mats[l, :LANES, :LANES] = m_re
        mats[l, :LANES, LANES:] = m_im
        mats[l, LANES:, :LANES] = -m_im
        mats[l, LANES:, LANES:] = m_re

    loop(0, layers, tables)

    def rows(v):
        return pl.ds(v * SUBLANES, SUBLANES)

    def take(buf, k, i, r):
        return buf[i, k, 0, r, :], buf[i, k, 1, r, :]

    def keep(buf, k, i, r, amp):
        buf[i, k, 0, r, :] = amp[0]
        buf[i, k, 1, r, :] = amp[1]

    def angles(l, lay, k):
        g = gam[l]

        def body(i):
            for v in range(per):
                t = g * cost[lay, i, k, rows(v), :]
                keep(trig, k, i, rows(v), (jnp.cos(t), jnp.sin(t)))

        loop(0, BLOCKS, body)

    def inner(buf, k, l):
        size = BLOCKS * per * SUBLANES
        x = jnp.concatenate([buf[:, k, 0].reshape(size, LANES), buf[:, k, 1].reshape(size, LANES)], axis=1)
        y = jnp.dot(x, mats[l], precision=lax.Precision.HIGHEST, preferred_element_type=jnp.float32)
        buf[:, k, 0] = y[:, :LANES].reshape(BLOCKS, per * SUBLANES, LANES)
        buf[:, k, 1] = y[:, LANES:].reshape(BLOCKS, per * SUBLANES, LANES)
        c, s = tabs[l, 0], tabs[l, 1]
        place = lax.broadcasted_iota(jnp.int32, (SUBLANES, LANES), 0)

        def partner(v, step):
            if 2 * step == SUBLANES:
                return pltpu.roll(v, step, 0)
            return jnp.where((place & step) != 0, pltpu.roll(v, step, 0), pltpu.roll(v, SUBLANES - step, 0))

        def body(g):
            for i in range(GROUP):
                i = g * GROUP + i
                amps = []
                for v in range(per):
                    re, im = take(buf, k, i, rows(v))
                    for step in (1, 2, 4):
                        pr, pi = partner(re, step), partner(im, step)
                        re, im = c * re + s * pi, c * im - s * pr
                    amps.append((re, im))
                for v, amp in enumerate(rx_list(amps, c, s)):
                    keep(buf, k, i, rows(v), amp)

        loop(0, BLOCKS // GROUP, body)

    def block_bits(l, k, get, dst):
        c, s = tabs[l, 0], tabs[l, 1]
        for v in range(per):
            amps = rx_list([get(i, rows(v)) for i in range(BLOCKS)], c, s)
            for i, amp in enumerate(amps):
                keep(dst, k, i, rows(v), amp)

    def chunk_pair(k0, k1, l):
        c, s = tabs[l, 0], tabs[l, 1]

        def body(i):
            for v in range(per):
                p0, p1 = rx_pair(take(work, k0, i, rows(v)), take(work, k1, i, rows(v)), c, s)
                keep(work, k0, i, rows(v), p0)
                keep(work, k1, i, rows(v), p1)

        loop(0, BLOCKS, body)

    def ship(group, p):
        lo, size = group
        part = pl.ds(lo, size)
        at = GROUPS.index(group)

        def one(i):
            j, dev = peer(i)
            put(send.at[j, part], recv.at[p, me, part], send_sem.at[at], recv_sem.at[p, at], dev).start()

        loop(0, 15, one)
        pltpu.make_async_copy(send.at[me, part], recv.at[p, me, part], recv_sem.at[p, at]).start()

    def sent():
        for at, (lo, size) in enumerate(GROUPS):
            part = send.at[pl.ds(0, BLOCKS - 1), pl.ds(lo, size)]
            pltpu.make_async_copy(part, part, send_sem.at[at]).wait()

    def arrived(group, p):
        lo, size = group
        part = recv.at[p, :, pl.ds(lo, size)]
        pltpu.make_async_copy(part, part, recv_sem.at[p, GROUPS.index(group)]).wait()

    def phased(k, get):
        def phased_get(i, r):
            (re, im), (co, si) = get(i, r), take(trig, k, i, r)
            return re * co + im * si, im * co - re * si

        return phased_get

    def collect(l, p, with_angles):
        def fetch(k):
            block_bits(l, k, lambda i, r: take(recv.at[p], k, i, r), work)

        def early(k):
            fetch(k)
            inner(work, k, l)

        for group in GROUPS:
            lo, size = group
            hi = lo + size
            if with_angles and lo in (0, half):
                loop(lo, lo + half, lambda k: angles(l + 1, 1 - p, k))
            arrived(group, p)
            if hi <= half:
                loop(lo, hi, early)
            else:
                loop(lo, hi, fetch)
            if hi == half:
                loop(0, 2, lambda i: chunk_pair(2 * i, 2 * i + 1, l))
                loop(0, 2, lambda i: chunk_pair(i, i + 2, l))
            if hi == n - 1:
                chunk_pair(4, 5, l)

    def first_chunk(l):
        c, s = tabs[l, 0], tabs[l, 1]

        def get(i, r):
            upper = rx_pair(take(work, 6, i, r), take(work, 7, i, r), c, s)[0]
            upper = rx_pair(take(work, 4, i, r), upper, c, s)[0]
            return rx_pair(take(work, 0, i, r), upper, c, s)[0]

        return get

    def rest(l):
        chunk_pair(6, 7, l)
        loop(0, 2, lambda i: chunk_pair(4 + i, 6 + i, l))

    def start(k, late):
        angles(0, 0, k)
        block_bits(0, k, lambda i, r: (trig[i, k, 0, r, :], -trig[i, k, 1, r, :]), send)
        if late:
            inner(send, k, 0)

    for group in GROUPS:
        lo, size = group
        loop(lo, lo + size, lambda k: start(k, lo >= half))
        ship(group, 0)

    pltpu.make_async_copy(cost.at[1], cost.at[1], crecv_sem).wait()
    part = cost.at[0, pl.ds(0, BLOCKS - 1)]
    pltpu.make_async_copy(part, part, csend_sem).wait()

    def layer(l):
        p = l % 2
        collect(l, p, True)
        sent()
        for group in GROUPS:
            lo, size = group
            if lo == 0:
                block_bits(l + 1, 0, phased(0, first_chunk(l)), send)
                ship(group, 1 - p)
                rest(l)
                loop(0, half, lambda k: chunk_pair(k, k + half, l))
                continue

            def resend(k):
                block_bits(l + 1, k, phased(k, lambda i, r: take(work, k, i, r)), send)
                if lo >= half:
                    inner(send, k, l + 1)

            loop(lo, lo + size, resend)
            ship(group, 1 - p)

    loop(0, layers - 1, layer)

    last = layers - 1
    collect(last, last % 2, False)
    rest(last)
    c, s = tabs[last, 0], tabs[last, 1]

    def finish(k, acc):
        def body(i, acc):
            for v in range(per):
                r = rows(v)
                pair = rx_pair(take(work, k, i, r), take(work, k + half, i, r), c, s)
                for kk, (re, im) in zip((k, k + half), pair):
                    keep(work, kk, i, r, (re, im))
                    acc = acc + cost[0, i, kk, r, :] * (re * re + im * im)
            return acc

        return lax.fori_loop(0, BLOCKS, body, acc)

    en_send[...] = lax.fori_loop(0, half, finish, jnp.zeros((SUBLANES, LANES), jnp.float32))
    loop(0, 15, lambda i: put(en_send, en_recv.at[me], esend_sem, erecv_sem, peer(i)[1]).start())
    pltpu.make_async_copy(en_send, en_recv.at[me], erecv_sem).start()
    sent()
    pltpu.make_async_copy(en_recv, en_recv, erecv_sem).wait()
    part = en_recv.at[pl.ds(0, BLOCKS - 1)]
    pltpu.make_async_copy(part, part, esend_sem).wait()
    full = en_recv[0]
    for i in range(1, BLOCKS):
        full = full + en_recv[i]
    en_out[0] = jnp.sum(full) / total


def split_kernel(pair, re_out, im_out, sem):
    copies = [pltpu.make_async_copy(pair.at[:, :, part], out, sem.at[part])
              for part, out in enumerate((re_out, im_out))]
    for copy in copies:
        copy.start()
    for copy in copies:
        copy.wait()


def solution(mesh):
    state_spec = P(("inst", "qx", "qy"))

    def device_body(cost_local, gammas, betas):
        local = cost_local.shape[0]
        vregs = local // (BLOCKS * SUBLANES * LANES)
        layers = gammas.shape[0]
        n = CHUNKS
        r = vregs // n * SUBLANES
        shape = (BLOCKS, n, r, LANES)
        pair = (BLOCKS, n, 2, r, LANES)
        f32 = jnp.float32
        any_spec = pl.BlockSpec(memory_space=pl.ANY)
        smem = pl.BlockSpec(memory_space=pltpu.SMEM)
        vmem = pl.BlockSpec(memory_space=pltpu.VMEM)
        dma = pltpu.SemaphoreType.DMA
        g = len(GROUPS)
        energy, state = pl.pallas_call(
            functools.partial(kernel, layers, vregs, float(local * BLOCKS)),
            out_shape=[jax.ShapeDtypeStruct((1,), f32), pltpu.VMEM(pair, f32)],
            in_specs=[any_spec, smem, smem],
            out_specs=[smem, vmem],
            scratch_shapes=[
                pltpu.VMEM((2,) + shape, f32),
                pltpu.VMEM(pair, f32),
                pltpu.VMEM((2,) + pair, f32),
                pltpu.VMEM(pair, f32),
                pltpu.VMEM((layers, 2 * LANES, 2 * LANES), f32),
                pltpu.VMEM((layers, 2, SUBLANES, LANES), f32),
                pltpu.VMEM((SUBLANES, LANES), f32),
                pltpu.VMEM((BLOCKS, SUBLANES, LANES), f32),
                dma, dma, dma, dma((g,)), dma((2, g)), dma, dma,
            ],
            compiler_params=pltpu.CompilerParams(collective_id=0, has_side_effects=True),
            name="qaoa",
        )(cost_local.reshape(shape), gammas, betas)
        out_re, out_im = pl.pallas_call(
            split_kernel,
            out_shape=[jax.ShapeDtypeStruct(shape, f32)] * 2,
            in_specs=[vmem],
            out_specs=[any_spec] * 2,
            scratch_shapes=[dma((2,))],
            name="split",
        )(pltpu.with_memory_space_constraint(state, pltpu.VMEM))
        return energy, out_re.reshape(local), out_im.reshape(local)

    return jax.shard_map(device_body, mesh=mesh, in_specs=(state_spec, P(), P()),
                         out_specs=(P("inst"), state_spec, state_spec), check_vma=False)
```

time: 325 us -> 319 us (0.982)
  local copies, waits for them, and re-layouts: 3.39 us -> 0 us
    pallas_call x1, Pallas kernels: 319 us -> 315 us  [device_body(): pl.pallas_call(functools.partial(kernel, layers, vregs, float(local * BLO...]
    unnamed x4 -> x0, local copies, waits for them, and re-layouts: 3.39 us -> none
where the time goes in v3:
time: 319 us
  Pallas kernels  317 us (99%)
    pallas_call x1, Pallas kernels, device_body(): pl.pallas_call(functools.partial(kernel, layers, vregs, float(local * BLO...  315 us

profile of v3, /device:TPU:0, one launch (start us, length us, event | category | flops | bytes accessed | tf_op | source)
XLA Modules:
  0.0 319.2 jit_solution(1163174629866710521)
XLA Ops:
  0.6 315.5 %qaoa.1 = (f32[1]{0:T(128)}, f32[16,8,2,16,128]{4,3,2,1,0:T(8,128)S(1)}) custom-call(f32[16,8,16,128]{3,2,1,0:T(8,128)} %bitcast.3, f32[6]{0:T(128)} %gam.1, f32[6]{0:T(128)} %bet.1), custom_call_target="tpu_custom_call" | custom-call | tf_op jit(solution)/shard_map/qaoa/pallas_call | solution.py:329
  316.1 1.3 split.1

commit v4 on v3

--- a/solution.py
+++ b/solution.py
@@ -73,7 +73,7 @@
         put(cost.at[0, j], cost.at[1, me], csend_sem, crecv_sem, dev).start()
 
     loop(0, 15, share)
-    pltpu.make_async_copy(cost.at[0, me], cost.at[1, me], crecv_sem).start()
+    cost[1, me] = cost[0, me]
 
     def tables(l):
         angle = jnp.full((SUBLANES, LANES), 0.5 * bet[l], jnp.float32)
@@ -172,19 +172,19 @@
 
         def one(i):
             j, dev = peer(i)
-            put(send.at[j, part], recv.at[p, me, part], send_sem.at[at], recv_sem.at[p, at], dev).start()
+            put(send.at[p, j, part], recv.at[p, me, part], send_sem.at[p, at], recv_sem.at[p, at], dev).start()
 
         loop(0, 15, one)
-        pltpu.make_async_copy(send.at[me, part], recv.at[p, me, part], recv_sem.at[p, at]).start()
-
-    def sent():
+        recv[p, me, part] = send[p, me, part]
+
+    def sent(p):
         for at, (lo, size) in enumerate(GROUPS):
-            part = send.at[pl.ds(0, BLOCKS - 1), pl.ds(lo, size)]
-            pltpu.make_async_copy(part, part, send_sem.at[at]).wait()
+            part = send.at[p, pl.ds(0, BLOCKS - 1), pl.ds(lo, size)]
+            pltpu.make_async_copy(part, part, send_sem.at[p, at]).wait()
 
     def arrived(group, p):
         lo, size = group
-        part = recv.at[p, :, pl.ds(lo, size)]
+        part = recv.at[p, pl.ds(0, BLOCKS - 1), pl.ds(lo, size)]
         pltpu.make_async_copy(part, part, recv_sem.at[p, GROUPS.index(group)]).wait()
 
     def phased(k, get):
@@ -234,36 +234,36 @@
 
     def start(k, late):
         angles(0, 0, k)
-        block_bits(0, k, lambda i, r: (trig[i, k, 0, r, :], -trig[i, k, 1, r, :]), send)
+        block_bits(0, k, lambda i, r: (trig[i, k, 0, r, :], -trig[i, k, 1, r, :]), send.at[0])
         if late:
-            inner(send, k, 0)
+            inner(send.at[0], k, 0)
 
     for group in GROUPS:
         lo, size = group
         loop(lo, lo + size, lambda k: start(k, lo >= half))
         ship(group, 0)
 
-    pltpu.make_async_copy(cost.at[1], cost.at[1], crecv_sem).wait()
     part = cost.at[0, pl.ds(0, BLOCKS - 1)]
+    pltpu.make_async_copy(part, part, crecv_sem).wait()
     pltpu.make_async_copy(part, part, csend_sem).wait()
 
     def layer(l):
         p = l % 2
+        pl.when(l > 0)(lambda: sent(1 - p))
         collect(l, p, True)
-        sent()
         for group in GROUPS:
             lo, size = group
             if lo == 0:
-                block_bits(l + 1, 0, phased(0, first_chunk(l)), send)
+                block_bits(l + 1, 0, phased(0, first_chunk(l)), send.at[1 - p])
                 ship(group, 1 - p)
                 rest(l)
                 loop(0, half, lambda k: chunk_pair(k, k + half, l))
                 continue
 
             def resend(k):
-                block_bits(l + 1, k, phased(k, lambda i, r: take(work, k, i, r)), send)
+                block_bits(l + 1, k, phased(k, lambda i, r: take(work, k, i, r)), send.at[1 - p])
                 if lo >= half:
-                    inner(send, k, l + 1)
+                    inner(send.at[1 - p], k, l + 1)
 
             loop(lo, lo + size, resend)
             ship(group, 1 - p)
@@ -289,10 +289,11 @@
 
     en_send[...] = lax.fori_loop(0, half, finish, jnp.zeros((SUBLANES, LANES), jnp.float32))
     loop(0, 15, lambda i: put(en_send, en_recv.at[me], esend_sem, erecv_sem, peer(i)[1]).start())
-    pltpu.make_async_copy(en_send, en_recv.at[me], erecv_sem).start()
-    sent()
-    pltpu.make_async_copy(en_recv, en_recv, erecv_sem).wait()
+    en_recv[me] = en_send[...]
     part = en_recv.at[pl.ds(0, BLOCKS - 1)]
+    sent(1 - last % 2)
+    sent(last % 2)
+    pltpu.make_async_copy(part, part, erecv_sem).wait()
     pltpu.make_async_copy(part, part, esend_sem).wait()
     full = en_recv[0]
     for i in range(1, BLOCKS):
@@ -335,12 +336,12 @@
                 pltpu.VMEM((2,) + shape, f32),
                 pltpu.VMEM(pair, f32),
                 pltpu.VMEM((2,) + pair, f32),
-                pltpu.VMEM(pair, f32),
+                pltpu.VMEM((2,) + pair, f32),
                 pltpu.VMEM((layers, 2 * LANES, 2 * LANES), f32),
                 pltpu.VMEM((layers, 2, SUBLANES, LANES), f32),
                 pltpu.VMEM((SUBLANES, LANES), f32),
                 pltpu.VMEM((BLOCKS, SUBLANES, LANES), f32),
-                dma, dma, dma, dma((g,)), dma((2, g)), dma, dma,
+                dma, dma, dma, dma((2, g)), dma((2, g)), dma, dma,
             ],
             compiler_params=pltpu.CompilerParams(collective_id=0, has_side_effects=True),
             name="qaoa",

time: 319 us -> 319 us (level)
  no operation moved by 1% of the time
where the time goes in v4:
time: 319 us
  Pallas kernels  316 us (99%)
    pallas_call x1, Pallas kernels, device_body(): pl.pallas_call(functools.partial(kernel, layers, vregs, float(local * BLO...  315 us

profile of v4, /device:TPU:0, one launch (start us, length us, event | category | flops | bytes accessed | tf_op | source)
XLA Modules:
  0.0 318.8 jit_solution(13074790371860081834)
XLA Ops:
  0.6 315.1 %qaoa.1 = (f32[1]{0:T(128)}, f32[16,8,2,16,128]{4,3,2,1,0:T(8,128)S(1)}) custom-call(f32[16,8,16,128]{3,2,1,0:T(8,128)} %bitcast.3, f32[6]{0:T(128)} %gam.1, f32[6]{0:T(128)} %bet.1), custom_call_target="tpu_custom_call" | custom-call | tf_op jit(solution)/shard_map/qaoa/pallas_call | solution.py:330
  315.7 1.3 split.1

commit v5 on v4

--- a/solution.py
+++ b/solution.py
@@ -11,7 +11,7 @@
 SUBLANES = 8
 BLOCKS = 16
 CHUNKS = 8
-GROUPS = ((0, 1), (1, 3), (4, 3), (7, 1))
+GROUPS = ((0, 2), (2, 2), (4, 2), (6, 2))
 GROUP = 4
 
 
@@ -208,23 +208,19 @@
             if with_angles and lo in (0, half):
                 loop(lo, lo + half, lambda k: angles(l + 1, 1 - p, k))
             arrived(group, p)
-            if hi <= half:
-                loop(lo, hi, early)
-            else:
-                loop(lo, hi, fetch)
+            loop(lo, hi, early if hi <= half else fetch)
+            if hi < n:
+                chunk_pair(lo, lo + 1, l)
             if hi == half:
-                loop(0, 2, lambda i: chunk_pair(2 * i, 2 * i + 1, l))
                 loop(0, 2, lambda i: chunk_pair(i, i + 2, l))
-            if hi == n - 1:
-                chunk_pair(4, 5, l)
-
-    def first_chunk(l):
+
+    def first_chunk(l, k):
         c, s = tabs[l, 0], tabs[l, 1]
 
         def get(i, r):
-            upper = rx_pair(take(work, 6, i, r), take(work, 7, i, r), c, s)[0]
-            upper = rx_pair(take(work, 4, i, r), upper, c, s)[0]
-            return rx_pair(take(work, 0, i, r), upper, c, s)[0]
+            upper = rx_pair(take(work, 6 + k, i, r), take(work, 7 - k, i, r), c, s)[0]
+            upper = rx_pair(take(work, 4 + k, i, r), upper, c, s)[0]
+            return rx_pair(take(work, k, i, r), upper, c, s)[0]
 
         return get
 
@@ -254,7 +250,7 @@
         for group in GROUPS:
             lo, size = group
             if lo == 0:
-                block_bits(l + 1, 0, phased(0, first_chunk(l)), send.at[1 - p])
+                loop(0, 2, lambda k: block_bits(l + 1, k, phased(k, first_chunk(l, k)), send.at[1 - p]))
                 ship(group, 1 - p)
                 rest(l)
                 loop(0, half, lambda k: chunk_pair(k, k + half, l))

time: 319 us -> 312 us (0.978)
  Pallas kernels: 316 us -> 310 us
    pallas_call x1, Pallas kernels: 315 us -> 308 us  [device_body(): pl.pallas_call(functools.partial(kernel, layers, vregs, float(local * BLO...]
where the time goes in v5:
time: 312 us
  Pallas kernels  310 us (99%)
    pallas_call x1, Pallas kernels, device_body(): pl.pallas_call(functools.partial(kernel, layers, vregs, float(local * BLO...  308 us

profile of v5, /device:TPU:0, one launch (start us, length us, event | category | flops | bytes accessed | tf_op | source)
XLA Modules:
  0.0 312.0 jit_solution(12853303244125704962)
XLA Ops:
  0.6 308.3 %qaoa.1 = (f32[1]{0:T(128)}, f32[16,8,2,16,128]{4,3,2,1,0:T(8,128)S(1)}) custom-call(f32[16,8,16,128]{3,2,1,0:T(8,128)} %bitcast.3, f32[6]{0:T(128)} %gam.1, f32[6]{0:T(128)} %bet.1), custom_call_target="tpu_custom_call" | custom-call | tf_op jit(solution)/shard_map/qaoa/pallas_call | solution.py:326
  308.9 1.3 split.1

commit v6 on v5

--- a/solution.py
+++ b/solution.py
@@ -36,8 +36,9 @@
 
 
 def kernel(layers, vregs, total, cost_in, gam, bet, en_out, work,
-           cost, trig, recv, send, mats, tabs, en_send, en_recv,
-           load_sem, csend_sem, crecv_sem, send_sem, recv_sem, esend_sem, erecv_sem):
+           cost, trig, recv, send, mats, tabs, en_send, en_recv, far_cost, far_send,
+           load_sem, csend_sem, crecv_sem, send_sem, recv_sem, esend_sem, erecv_sem,
+           fsend_sem, frecv_sem, xsend_sem, xrecv_sem, pcsend_sem, psend_sem):
     n = CHUNKS
     half = n // 2
     per = vregs // n
@@ -68,11 +69,19 @@
     pl.semaphore_wait(barrier, 15)
     load.wait()
 
-    def share(i):
-        j, dev = peer(i)
-        put(cost.at[0, j], cost.at[1, me], csend_sem, crecv_sem, dev).start()
-
-    loop(0, 15, share)
+    half_z = b // 2
+    proxy_role = (b + 1) // 2 == 1
+    flips = [flip(a, m) for m in range(4)], [b, flip(b, 1)]
+    near = []
+    for mz, mx in ((1, 3), (1, 2), (1, 1), (1, 0), (0, 3), (0, 2), (0, 1)):
+        pa, pb = flips[0][mx], flips[1][mz]
+        near.append((pa * 4 + pb, {"qx": pa, "qy": pb}))
+
+    def cross(k):
+        return put(cost.at[0, :, k], far_cost.at[b % 2, :, k], xsend_sem.at[k], xrecv_sem.at[b % 2, k],
+                   {"qx": a, "qy": 2 - half_z})
+
+    cross(0).start()
     cost[1, me] = cost[0, me]
 
     def tables(l):
@@ -108,13 +117,13 @@
         buf[i, k, 0, r, :] = amp[0]
         buf[i, k, 1, r, :] = amp[1]
 
-    def angles(l, lay, k):
+    def angles(l, src, dst, k):
         g = gam[l]
 
         def body(i):
             for v in range(per):
-                t = g * cost[lay, i, k, rows(v), :]
-                keep(trig, k, i, rows(v), (jnp.cos(t), jnp.sin(t)))
+                t = g * src[i, k, rows(v), :]
+                keep(dst, k, i, rows(v), (jnp.cos(t), jnp.sin(t)))
 
         loop(0, BLOCKS, body)
 
@@ -194,7 +203,7 @@
 
         return phased_get
 
-    def collect(l, p, with_angles):
+    def collect(l, p):
         def fetch(k):
             block_bits(l, k, lambda i, r: take(recv.at[p], k, i, r), work)
 
@@ -205,8 +214,9 @@
         for group in GROUPS:
             lo, size = group
             hi = lo + size
-            if with_angles and lo in (0, half):
-                loop(lo, lo + half, lambda k: angles(l + 1, 1 - p, k))
+            if lo in (0, half):
+                pl.when(l < layers - 1)(
+                    lambda: loop(lo, lo + half, lambda k: angles(l + 1, cost.at[1 - p], trig, k)))
             arrived(group, p)
             loop(lo, hi, early if hi <= half else fetch)
             if hi < n:
@@ -228,25 +238,77 @@
         chunk_pair(6, 7, l)
         loop(0, 2, lambda i: chunk_pair(4 + i, 6 + i, l))
 
-    def start(k, late):
-        angles(0, 0, k)
-        block_bits(0, k, lambda i, r: (trig[i, k, 0, r, :], -trig[i, k, 1, r, :]), send.at[0])
-        if late:
-            inner(send.at[0], k, 0)
-
-    for group in GROUPS:
-        lo, size = group
-        loop(lo, lo + size, lambda k: start(k, lo >= half))
-        ship(group, 0)
-
-    part = cost.at[0, pl.ds(0, BLOCKS - 1)]
-    pltpu.make_async_copy(part, part, crecv_sem).wait()
+    def first(trig_ref, k):
+        return lambda i, r: (trig_ref[i, k, 0, r, :], -trig_ref[i, k, 1, r, :])
+
+    def start(k):
+        for j, dev in near:
+            put(cost.at[0, j, k], cost.at[1, me, k], csend_sem, crecv_sem.at[k], dev).start()
+        angles(0, cost.at[0], trig, k)
+        block_bits(0, k, first(trig, k), send.at[0])
+        for j, dev in near:
+            put(send.at[0, j, k], recv.at[0, me, k], fsend_sem.at[k], frecv_sem.at[k], dev).start()
+        recv[0, me, k] = send[0, me, k]
+        pl.when(k < n - 1)(lambda: cross(k + 1).start())
+
+    def proxy(k):
+        def one(x):
+            s = a * 4 + 2 * (1 - half_z) + x
+            pltpu.make_async_copy(far_cost.at[x, :, k], far_cost.at[x, :, k], xrecv_sem.at[x, k]).wait()
+            for j, dev in near:
+                put(far_cost.at[x, j, k], cost.at[1, s, k], pcsend_sem, crecv_sem.at[k], dev).start()
+            pltpu.make_async_copy(far_cost.at[x, me, k], cost.at[1, s, k], crecv_sem.at[k]).start()
+            angles(0, far_cost.at[x], far_send.at[x], k)
+            block_bits(0, k, first(far_send.at[x], k), far_send.at[x])
+            for j, dev in near:
+                put(far_send.at[x, j, k], recv.at[0, s, k], psend_sem.at[k], frecv_sem.at[k], dev).start()
+            pltpu.make_async_copy(far_send.at[x, me, k], recv.at[0, s, k], frecv_sem.at[k]).start()
+
+        loop(0, 2, one)
+
+    def first_collect(k):
+        part = cost.at[0, pl.ds(0, BLOCKS - 1), k]
+        pltpu.make_async_copy(part, part, crecv_sem.at[k]).wait()
+        angles(1, cost.at[1], trig, k)
+        part = recv.at[0, pl.ds(0, BLOCKS - 1), k]
+        pltpu.make_async_copy(part, part, frecv_sem.at[k]).wait()
+        block_bits(0, k, lambda i, r: take(recv.at[0], k, i, r), work)
+        inner(work, k, 0)
+
+    loop(0, n, start)
+
+    def step(k):
+        pl.when(proxy_role)(lambda: proxy(k))
+        pl.when(k > 0)(lambda: first_collect(k - 1))
+
+    loop(0, n, step)
+    first_collect(n - 1)
+    loop(0, 3, lambda i: chunk_pair(2 * i, 2 * i + 1, 0))
+    loop(0, 2, lambda i: chunk_pair(i, i + 2, 0))
+
+    def first_sent(k):
+        pltpu.make_async_copy(cost.at[0, :, k], cost.at[0, :, k], xsend_sem.at[k]).wait()
+        part = send.at[0, pl.ds(0, len(near)), k]
+        pltpu.make_async_copy(part, part, fsend_sem.at[k]).wait()
+
+    loop(0, n, first_sent)
+    part = cost.at[0, pl.ds(0, len(near))]
     pltpu.make_async_copy(part, part, csend_sem).wait()
+
+    @pl.when(proxy_role)
+    def _():
+        part = cost.at[0, pl.ds(0, 2 * len(near))]
+        pltpu.make_async_copy(part, part, pcsend_sem).wait()
+
+        def one(k):
+            part = recv.at[0, pl.ds(0, 2 * len(near)), k]
+            pltpu.make_async_copy(part, part, psend_sem.at[k]).wait()
+
+        loop(0, n, one)
 
     def layer(l):
         p = l % 2
-        pl.when(l > 0)(lambda: sent(1 - p))
-        collect(l, p, True)
+        pl.when(l > 1)(lambda: sent(1 - p))
         for group in GROUPS:
             lo, size = group
             if lo == 0:
@@ -263,11 +325,11 @@
 
             loop(lo, lo + size, resend)
             ship(group, 1 - p)
+        collect(l + 1, 1 - p)
 
     loop(0, layers - 1, layer)
 
     last = layers - 1
-    collect(last, last % 2, False)
     rest(last)
     c, s = tabs[last, 0], tabs[last, 1]
 
@@ -337,7 +399,10 @@
                 pltpu.VMEM((layers, 2, SUBLANES, LANES), f32),
                 pltpu.VMEM((SUBLANES, LANES), f32),
                 pltpu.VMEM((BLOCKS, SUBLANES, LANES), f32),
-                dma, dma, dma, dma((2, g)), dma((2, g)), dma, dma,
+                pltpu.VMEM((2,) + shape, f32),
+                pltpu.VMEM((2,) + pair, f32),
+                dma, dma, dma((n,)), dma((2, g)), dma((2, g)), dma, dma,
+                dma((n,)), dma((n,)), dma((n,)), dma((2, n)), dma, dma((n,)),
             ],
             compiler_params=pltpu.CompilerParams(collective_id=0, has_side_effects=True),
             name="qaoa",

time: 312 us -> 300 us (0.962)
  Pallas kernels: 310 us -> 297 us
    pallas_call x1, Pallas kernels: 308 us -> 296 us  [device_body(): pl.pallas_call(functools.partial(kernel, layers, vregs, float(local * BLO...]
where the time goes in v6:
time: 300 us
  Pallas kernels  297 us (99%)
    pallas_call x1, Pallas kernels, device_body(): pl.pallas_call(functools.partial(kernel, layers, vregs, float(local * BLO...  296 us

profile of v6, /device:TPU:0, one launch (start us, length us, event | category | flops | bytes accessed | tf_op | source)
XLA Modules:
  0.0 299.8 jit_solution(5983594272764740162)
XLA Ops:
  0.6 296.0 %qaoa.1 = (f32[1]{0:T(128)}, f32[16,8,2,16,128]{4,3,2,1,0:T(8,128)S(1)}) custom-call(f32[16,8,16,128]{3,2,1,0:T(8,128)} %bitcast.3, f32[6]{0:T(128)} %gam.1, f32[6]{0:T(128)} %bet.1), custom_call_target="tpu_custom_call" | custom-call | tf_op jit(solution)/shard_map/qaoa/pallas_call | solution.py:388
  296.7 1.3 split.1

commit v7 on v6

--- a/solution.py
+++ b/solution.py
@@ -52,10 +52,12 @@
 
         lax.fori_loop(lo, hi, step, 0)
 
-    def peer(i):
-        m = 15 - i
-        pa, pb = flip(a, m % 4), flip(b, m // 4)
-        return pa * 4 + pb, {"qx": pa, "qy": pb}
+    flips = [[flip(x, m) for m in range(4)] for x in (a, b)]
+    peers = []
+    for mz, mx in ((m // 4, m % 4) for m in range(15, 0, -1)):
+        pa, pb = flips[0][mx], flips[1][mz]
+        peers.append((pa * 4 + pb, {"qx": pa, "qy": pb}))
+    near = peers[8:]
 
     def put(src, dst, send_s, recv_s, dev):
         return pltpu.make_async_remote_copy(src, dst, send_s, recv_s, device_id=dev,
@@ -64,19 +66,14 @@
     load = pltpu.make_async_copy(cost_in, cost.at[0], load_sem)
     load.start()
     barrier = pltpu.get_barrier_semaphore()
-    loop(0, 15, lambda i: pl.semaphore_signal(barrier, inc=1, device_id=peer(i)[1],
-                                              device_id_type=pl.DeviceIdType.MESH))
+    for _, dev in peers:
+        pl.semaphore_signal(barrier, inc=1, device_id=dev, device_id_type=pl.DeviceIdType.MESH)
     pl.semaphore_wait(barrier, 15)
     load.wait()
 
     half_z = b // 2
-    proxy_role = (b + 1) // 2 == 1
-    flips = [flip(a, m) for m in range(4)], [b, flip(b, 1)]
-    near = []
-    for mz, mx in ((1, 3), (1, 2), (1, 1), (1, 0), (0, 3), (0, 2), (0, 1)):
-        pa, pb = flips[0][mx], flips[1][mz]
-        near.append((pa * 4 + pb, {"qx": pa, "qy": pb}))
-
+    role = (b + 1) // 2 % 2
+    proxy_role = role == 1
     def cross(k):
         return put(cost.at[0, :, k], far_cost.at[b % 2, :, k], xsend_sem.at[k], xrecv_sem.at[b % 2, k],
                    {"qx": a, "qy": 2 - half_z})
@@ -179,11 +176,8 @@
         part = pl.ds(lo, size)
         at = GROUPS.index(group)
 
-        def one(i):
-            j, dev = peer(i)
+        for j, dev in peers:
             put(send.at[p, j, part], recv.at[p, me, part], send_sem.at[p, at], recv_sem.at[p, at], dev).start()
-
-        loop(0, 15, one)
         recv[p, me, part] = send[p, me, part]
 
     def sent(p):
@@ -249,7 +243,8 @@
         for j, dev in near:
             put(send.at[0, j, k], recv.at[0, me, k], fsend_sem.at[k], frecv_sem.at[k], dev).start()
         recv[0, me, k] = send[0, me, k]
-        pl.when(k < n - 1)(lambda: cross(k + 1).start())
+        outer_ahead = (1 - role) * (n - 1) + role
+        pl.when(k < outer_ahead)(lambda: cross(k + 1).start())
 
     def proxy(k):
         def one(x):
@@ -265,6 +260,7 @@
             pltpu.make_async_copy(far_send.at[x, me, k], recv.at[0, s, k], frecv_sem.at[k]).start()
 
         loop(0, 2, one)
+        pl.when(k < n - 2)(lambda: cross(k + 2).start())
 
     def first_collect(k):
         part = cost.at[0, pl.ds(0, BLOCKS - 1), k]
@@ -346,7 +342,8 @@
         return lax.fori_loop(0, BLOCKS, body, acc)
 
     en_send[...] = lax.fori_loop(0, half, finish, jnp.zeros((SUBLANES, LANES), jnp.float32))
-    loop(0, 15, lambda i: put(en_send, en_recv.at[me], esend_sem, erecv_sem, peer(i)[1]).start())
+    for _, dev in peers:
+        put(en_send, en_recv.at[me], esend_sem, erecv_sem, dev).start()
     en_recv[me] = en_send[...]
     part = en_recv.at[pl.ds(0, BLOCKS - 1)]
     sent(1 - last % 2)

time: 300 us -> 299 us (level)
  no operation moved by 1% of the time
where the time goes in v7:
time: 299 us
  Pallas kernels  297 us (99%)
    pallas_call x1, Pallas kernels, device_body(): pl.pallas_call(functools.partial(kernel, layers, vregs, float(local * BLO...  295 us

profile of v7, /device:TPU:0, one launch (start us, length us, event | category | flops | bytes accessed | tf_op | source)
XLA Modules:
  0.0 299.2 jit_solution(4197828431928553568)
XLA Ops:
  0.6 295.4 %qaoa.1 = (f32[1]{0:T(128)}, f32[16,8,2,16,128]{4,3,2,1,0:T(8,128)S(1)}) custom-call(f32[16,8,16,128]{3,2,1,0:T(8,128)} %bitcast.3, f32[6]{0:T(128)} %gam.1, f32[6]{0:T(128)} %bet.1), custom_call_target="tpu_custom_call" | custom-call | tf_op jit(solution)/shard_map/qaoa/pallas_call | solution.py:385
  296.1 1.3 split.1

commit v8 on v7

--- a/solution.py
+++ b/solution.py
@@ -38,7 +38,7 @@
 def kernel(layers, vregs, total, cost_in, gam, bet, en_out, work,
            cost, trig, recv, send, mats, tabs, en_send, en_recv, far_cost, far_send,
            load_sem, csend_sem, crecv_sem, send_sem, recv_sem, esend_sem, erecv_sem,
-           fsend_sem, frecv_sem, xsend_sem, xrecv_sem, pcsend_sem, psend_sem):
+           fsend_sem, frecv_sem, xsend_sem, xrecv_sem, pcsend_sem, psend_sem, nrecv_sem, ready_sem):
     n = CHUNKS
     half = n // 2
     per = vregs // n
@@ -66,9 +66,20 @@
     load = pltpu.make_async_copy(cost_in, cost.at[0], load_sem)
     load.start()
     barrier = pltpu.get_barrier_semaphore()
-    for _, dev in peers:
-        pl.semaphore_signal(barrier, inc=1, device_id=dev, device_id_type=pl.DeviceIdType.MESH)
-    pl.semaphore_wait(barrier, 15)
+    half_z = b // 2
+    role = (b + 1) // 2 % 2
+    proxy_role = role == 1
+
+    def signal(sem, dev):
+        pl.semaphore_signal(sem, inc=1, device_id=dev, device_id_type=pl.DeviceIdType.MESH)
+
+    for _, dev in near:
+        signal(barrier, dev)
+    signal(barrier, {"qx": a, "qy": 2 - half_z})
+    pl.when(proxy_role)(lambda: signal(barrier, {"qx": a, "qy": 3 - 3 * half_z}))
+    pl.semaphore_wait(barrier, 8 + role)
+    for _, dev in near:
+        signal(ready_sem, dev)
     load.wait()
 
     half_z = b // 2
@@ -79,6 +90,8 @@
                    {"qx": a, "qy": 2 - half_z})
 
     cross(0).start()
+    for j, dev in near:
+        put(cost.at[0, j], cost.at[1, me], csend_sem, nrecv_sem, dev).start()
     cost[1, me] = cost[0, me]
 
     def tables(l):
@@ -235,16 +248,18 @@
     def first(trig_ref, k):
         return lambda i, r: (trig_ref[i, k, 0, r, :], -trig_ref[i, k, 1, r, :])
 
-    def start(k):
-        for j, dev in near:
-            put(cost.at[0, j, k], cost.at[1, me, k], csend_sem, crecv_sem.at[k], dev).start()
+    def start(k, targets):
+        if targets is peers:
+            pl.semaphore_wait(ready_sem, len(near))
+            for j, dev in peers[:8]:
+                put(cost.at[0, j, k], cost.at[1, me, k], csend_sem, crecv_sem.at[k], dev).start()
         angles(0, cost.at[0], trig, k)
         block_bits(0, k, first(trig, k), send.at[0])
-        for j, dev in near:
+        if targets is peers:
+            inner(send.at[0], k, 0)
+        for j, dev in targets:
             put(send.at[0, j, k], recv.at[0, me, k], fsend_sem.at[k], frecv_sem.at[k], dev).start()
         recv[0, me, k] = send[0, me, k]
-        outer_ahead = (1 - role) * (n - 1) + role
-        pl.when(k < outer_ahead)(lambda: cross(k + 1).start())
 
     def proxy(k):
         def one(x):
@@ -260,47 +275,63 @@
             pltpu.make_async_copy(far_send.at[x, me, k], recv.at[0, s, k], frecv_sem.at[k]).start()
 
         loop(0, 2, one)
-        pl.when(k < n - 2)(lambda: cross(k + 2).start())
-
-    def first_collect(k):
-        part = cost.at[0, pl.ds(0, BLOCKS - 1), k]
+
+    def first_collect(k, last=False):
+        part = cost.at[0, pl.ds(0, 8), k]
         pltpu.make_async_copy(part, part, crecv_sem.at[k]).wait()
         angles(1, cost.at[1], trig, k)
+        if last:
+            chunk_pair(4, 5, 0)
+            loop(0, 2, lambda i: chunk_pair(2 * i, 2 * i + 1, 0))
+            loop(0, 2, lambda i: chunk_pair(i, i + 2, 0))
         part = recv.at[0, pl.ds(0, BLOCKS - 1), k]
         pltpu.make_async_copy(part, part, frecv_sem.at[k]).wait()
         block_bits(0, k, lambda i, r: take(recv.at[0], k, i, r), work)
-        inner(work, k, 0)
-
-    loop(0, n, start)
+        if not last:
+            inner(work, k, 0)
+
+    def begin(k):
+        start(k, near)
+        pl.when(k < n - 2)(lambda: cross(k + 1).start())
+
+    loop(0, n - 1, begin)
+    start(n - 1, peers)
 
     def step(k):
         pl.when(proxy_role)(lambda: proxy(k))
+
+        @pl.when(k == 1)
+        def _():
+            part = cost.at[0, pl.ds(0, len(near))]
+            pltpu.make_async_copy(part, part, nrecv_sem).wait()
+
         pl.when(k > 0)(lambda: first_collect(k - 1))
 
-    loop(0, n, step)
-    first_collect(n - 1)
-    loop(0, 3, lambda i: chunk_pair(2 * i, 2 * i + 1, 0))
-    loop(0, 2, lambda i: chunk_pair(i, i + 2, 0))
+    loop(0, n - 1, step)
+    first_collect(n - 2)
+    first_collect(n - 1, True)
 
     def first_sent(k):
         pltpu.make_async_copy(cost.at[0, :, k], cost.at[0, :, k], xsend_sem.at[k]).wait()
         part = send.at[0, pl.ds(0, len(near)), k]
         pltpu.make_async_copy(part, part, fsend_sem.at[k]).wait()
 
-    loop(0, n, first_sent)
-    part = cost.at[0, pl.ds(0, len(near))]
+    loop(0, n - 1, first_sent)
+    part = send.at[0, pl.ds(0, len(peers)), n - 1]
+    pltpu.make_async_copy(part, part, fsend_sem.at[n - 1]).wait()
+    part = cost.at[0, pl.ds(0, (len(near) * (n - 1) + len(peers)) // n)]
     pltpu.make_async_copy(part, part, csend_sem).wait()
 
     @pl.when(proxy_role)
     def _():
-        part = cost.at[0, pl.ds(0, 2 * len(near))]
+        part = cost.at[0, pl.ds(0, 2 * len(near)), pl.ds(0, n - 1)]
         pltpu.make_async_copy(part, part, pcsend_sem).wait()
 
         def one(k):
             part = recv.at[0, pl.ds(0, 2 * len(near)), k]
             pltpu.make_async_copy(part, part, psend_sem.at[k]).wait()
 
-        loop(0, n, one)
+        loop(0, n - 1, one)
 
     def layer(l):
         p = l % 2
@@ -326,22 +357,20 @@
     loop(0, layers - 1, layer)
 
     last = layers - 1
-    rest(last)
     c, s = tabs[last, 0], tabs[last, 1]
 
-    def finish(k, acc):
-        def body(i, acc):
-            for v in range(per):
-                r = rows(v)
-                pair = rx_pair(take(work, k, i, r), take(work, k + half, i, r), c, s)
-                for kk, (re, im) in zip((k, k + half), pair):
-                    keep(work, kk, i, r, (re, im))
-                    acc = acc + cost[0, i, kk, r, :] * (re * re + im * im)
-            return acc
-
-        return lax.fori_loop(0, BLOCKS, body, acc)
-
-    en_send[...] = lax.fori_loop(0, half, finish, jnp.zeros((SUBLANES, LANES), jnp.float32))
+    def finish(i, acc):
+        for v in range(per):
+            r = rows(v)
+            amps = [take(work, k, i, r) for k in range(n)]
+            for k0, k1 in ((6, 7), (4, 6), (5, 7), (0, 4), (1, 5), (2, 6), (3, 7)):
+                amps[k0], amps[k1] = rx_pair(amps[k0], amps[k1], c, s)
+            for k, (re, im) in enumerate(amps):
+                keep(work, k, i, r, (re, im))
+                acc = acc + cost[0, i, k, r, :] * (re * re + im * im)
+        return acc
+
+    en_send[...] = lax.fori_loop(0, BLOCKS, finish, jnp.zeros((SUBLANES, LANES), jnp.float32))
     for _, dev in peers:
         put(en_send, en_recv.at[me], esend_sem, erecv_sem, dev).start()
     en_recv[me] = en_send[...]
@@ -399,7 +428,8 @@
                 pltpu.VMEM((2,) + shape, f32),
                 pltpu.VMEM((2,) + pair, f32),
                 dma, dma, dma((n,)), dma((2, g)), dma((2, g)), dma, dma,
-                dma((n,)), dma((n,)), dma((n,)), dma((2, n)), dma, dma((n,)),
+                dma((n,)), dma((n,)), dma((n,)), dma((2, n)), dma, dma((n,)), dma,
+                pltpu.SemaphoreType.REGULAR,
             ],
             compiler_params=pltpu.CompilerParams(collective_id=0, has_side_effects=True),
             name="qaoa",

time: 299 us -> 298 us (level)
  no operation moved by 1% of the time
where the time goes in v8:
time: 298 us
  Pallas kernels  295 us (99%)
    pallas_call x1, Pallas kernels, device_body(): pl.pallas_call(functools.partial(kernel, layers, vregs, float(local * BLO...  294 us

profile of v8, /device:TPU:0, one launch (start us, length us, event | category | flops | bytes accessed | tf_op | source)
XLA Modules:
  0.0 297.6 jit_solution(544596634882230474)
XLA Ops:
  0.6 293.9 %qaoa.1 = (f32[1]{0:T(128)}, f32[16,8,2,16,128]{4,3,2,1,0:T(8,128)S(1)}) custom-call(f32[16,8,16,128]{3,2,1,0:T(8,128)} %bitcast.3, f32[6]{0:T(128)} %gam.1, f32[6]{0:T(128)} %bet.1), custom_call_target="tpu_custom_call" | custom-call | tf_op jit(solution)/shard_map/qaoa/pallas_call | solution.py:414
  294.5 1.3 split.1

commit v9 on v8

--- a/solution.py
+++ b/solution.py
@@ -121,11 +121,16 @@
         return pl.ds(v * SUBLANES, SUBLANES)
 
     def take(buf, k, i, r):
+        if buf is work:
+            return buf[0, i, k, r, :], buf[1, i, k, r, :]
         return buf[i, k, 0, r, :], buf[i, k, 1, r, :]
 
     def keep(buf, k, i, r, amp):
-        buf[i, k, 0, r, :] = amp[0]
-        buf[i, k, 1, r, :] = amp[1]
+        for part in range(2):
+            if buf is work:
+                buf[part, i, k, r, :] = amp[part]
+            else:
+                buf[i, k, part, r, :] = amp[part]
 
     def angles(l, src, dst, k):
         g = gam[l]
@@ -139,10 +144,11 @@
 
     def inner(buf, k, l):
         size = BLOCKS * per * SUBLANES
-        x = jnp.concatenate([buf[:, k, 0].reshape(size, LANES), buf[:, k, 1].reshape(size, LANES)], axis=1)
+        re_at, im_at = [(part, slice(None), k) if buf is work else (slice(None), k, part) for part in range(2)]
+        x = jnp.concatenate([buf[re_at].reshape(size, LANES), buf[im_at].reshape(size, LANES)], axis=1)
         y = jnp.dot(x, mats[l], precision=lax.Precision.HIGHEST, preferred_element_type=jnp.float32)
-        buf[:, k, 0] = y[:, :LANES].reshape(BLOCKS, per * SUBLANES, LANES)
-        buf[:, k, 1] = y[:, LANES:].reshape(BLOCKS, per * SUBLANES, LANES)
+        buf[re_at] = y[:, :LANES].reshape(BLOCKS, per * SUBLANES, LANES)
+        buf[im_at] = y[:, LANES:].reshape(BLOCKS, per * SUBLANES, LANES)
         c, s = tabs[l, 0], tabs[l, 1]
         place = lax.broadcasted_iota(jnp.int32, (SUBLANES, LANES), 0)
 
@@ -316,25 +322,27 @@
         part = send.at[0, pl.ds(0, len(near)), k]
         pltpu.make_async_copy(part, part, fsend_sem.at[k]).wait()
 
-    loop(0, n - 1, first_sent)
-    part = send.at[0, pl.ds(0, len(peers)), n - 1]
-    pltpu.make_async_copy(part, part, fsend_sem.at[n - 1]).wait()
-    part = cost.at[0, pl.ds(0, (len(near) * (n - 1) + len(peers)) // n)]
-    pltpu.make_async_copy(part, part, csend_sem).wait()
-
-    @pl.when(proxy_role)
-    def _():
-        part = cost.at[0, pl.ds(0, 2 * len(near)), pl.ds(0, n - 1)]
-        pltpu.make_async_copy(part, part, pcsend_sem).wait()
-
-        def one(k):
-            part = recv.at[0, pl.ds(0, 2 * len(near)), k]
-            pltpu.make_async_copy(part, part, psend_sem.at[k]).wait()
-
-        loop(0, n - 1, one)
+    def first_sends():
+        loop(0, n - 1, first_sent)
+        part = send.at[0, pl.ds(0, len(peers)), n - 1]
+        pltpu.make_async_copy(part, part, fsend_sem.at[n - 1]).wait()
+        part = cost.at[0, pl.ds(0, (len(near) * (n - 1) + len(peers)) // n)]
+        pltpu.make_async_copy(part, part, csend_sem).wait()
+
+        @pl.when(proxy_role)
+        def _():
+            part = cost.at[0, pl.ds(0, 2 * len(near)), pl.ds(0, n - 1)]
+            pltpu.make_async_copy(part, part, pcsend_sem).wait()
+
+            def one(k):
+                part = recv.at[0, pl.ds(0, 2 * len(near)), k]
+                pltpu.make_async_copy(part, part, psend_sem.at[k]).wait()
+
+            loop(0, n - 1, one)
 
     def layer(l):
         p = l % 2
+        pl.when(l == 1)(first_sends)
         pl.when(l > 1)(lambda: sent(1 - p))
         for group in GROUPS:
             lo, size = group
@@ -386,7 +394,7 @@
 
 
 def split_kernel(pair, re_out, im_out, sem):
-    copies = [pltpu.make_async_copy(pair.at[:, :, part], out, sem.at[part])
+    copies = [pltpu.make_async_copy(pair.at[part], out, sem.at[part])
               for part, out in enumerate((re_out, im_out))]
     for copy in copies:
         copy.start()
@@ -413,7 +421,7 @@
         g = len(GROUPS)
         energy, state = pl.pallas_call(
             functools.partial(kernel, layers, vregs, float(local * BLOCKS)),
-            out_shape=[jax.ShapeDtypeStruct((1,), f32), pltpu.VMEM(pair, f32)],
+            out_shape=[jax.ShapeDtypeStruct((1,), f32), pltpu.VMEM((2,) + shape, f32)],
             in_specs=[any_spec, smem, smem],
             out_specs=[smem, vmem],
             scratch_shapes=[

time: 298 us -> 297 us (level)
  no operation moved by 1% of the time
where the time goes in v9:
time: 297 us
  Pallas kernels  295 us (99%)
    pallas_call x1, Pallas kernels, device_body(): pl.pallas_call(functools.partial(kernel, layers, vregs, float(local * BLO...  293 us

profile of v9, /device:TPU:0, one launch (start us, length us, event | category | flops | bytes accessed | tf_op | source)
XLA Modules:
  0.0 297.0 jit_solution(11880026269422798234)
XLA Ops:
  0.6 293.3 %qaoa.1 = (f32[1]{0:T(128)}, f32[2,16,8,16,128]{4,3,2,1,0:T(8,128)S(1)}) custom-call(f32[16,8,16,128]{3,2,1,0:T(8,128)} %bitcast.3, f32[6]{0:T(128)} %gam.1, f32[6]{0:T(128)} %bet.1), custom_call_target="tpu_custom_call" | custom-call | tf_op jit(solution)/shard_map/qaoa/pallas_call | solution.py:422
  293.9 1.3 split.1

commit v10 on v9

--- a/solution.py
+++ b/solution.py
@@ -268,19 +268,21 @@
         recv[0, me, k] = send[0, me, k]
 
     def proxy(k):
+        both = pl.ds(a * 4 + 2 * (1 - half_z), 2)
+        for x in range(2):
+            pltpu.make_async_copy(far_cost.at[x, :, k], far_cost.at[x, :, k], xrecv_sem.at[x, k]).wait()
+        for j, dev in near:
+            put(far_cost.at[:, j, k], cost.at[1, both, k], pcsend_sem, crecv_sem.at[k], dev).start()
+        pltpu.make_async_copy(far_cost.at[:, me, k], cost.at[1, both, k], crecv_sem.at[k]).start()
+
         def one(x):
-            s = a * 4 + 2 * (1 - half_z) + x
-            pltpu.make_async_copy(far_cost.at[x, :, k], far_cost.at[x, :, k], xrecv_sem.at[x, k]).wait()
-            for j, dev in near:
-                put(far_cost.at[x, j, k], cost.at[1, s, k], pcsend_sem, crecv_sem.at[k], dev).start()
-            pltpu.make_async_copy(far_cost.at[x, me, k], cost.at[1, s, k], crecv_sem.at[k]).start()
             angles(0, far_cost.at[x], far_send.at[x], k)
             block_bits(0, k, first(far_send.at[x], k), far_send.at[x])
-            for j, dev in near:
-                put(far_send.at[x, j, k], recv.at[0, s, k], psend_sem.at[k], frecv_sem.at[k], dev).start()
-            pltpu.make_async_copy(far_send.at[x, me, k], recv.at[0, s, k], frecv_sem.at[k]).start()
 
         loop(0, 2, one)
+        for j, dev in near:
+            put(far_send.at[:, j, k], recv.at[0, both, k], psend_sem.at[k], frecv_sem.at[k], dev).start()
+        pltpu.make_async_copy(far_send.at[:, me, k], recv.at[0, both, k], frecv_sem.at[k]).start()
 
     def first_collect(k, last=False):
         part = cost.at[0, pl.ds(0, 8), k]

time: 297 us -> 298 us (level)
  no operation moved by 1% of the time
where the time goes in v10:
time: 298 us; the launch traced here: 297 us
  Pallas kernels  295 us (99%)
    pallas_call x1, Pallas kernels, device_body(): pl.pallas_call(functools.partial(kernel, layers, vregs, float(local * BLO...  294 us

profile of v10, /device:TPU:0, one launch (start us, length us, event | category | flops | bytes accessed | tf_op | source)
XLA Modules:
  0.0 297.5 jit_solution(16384522482994086635)
XLA Ops:
  0.6 293.8 %qaoa.1 = (f32[1]{0:T(128)}, f32[2,16,8,16,128]{4,3,2,1,0:T(8,128)S(1)}) custom-call(f32[16,8,16,128]{3,2,1,0:T(8,128)} %bitcast.3, f32[6]{0:T(128)} %gam.1, f32[6]{0:T(128)} %bet.1), custom_call_target="tpu_custom_call" | custom-call | tf_op jit(solution)/shard_map/qaoa/pallas_call | solution.py:424
  294.4 1.3 split.1
